TPU v7x, 32 devices: a whole 2x2x4 slice. The times are simulated.
32 devices in a mesh: grp: 2 (over x), tm: 16 (over z, y, core).
Axes of the slice: x: 2, y: 2, z: 4, core: 2. Of those that a mesh axis runs over, the one named last changes fastest.
Arguments:
- video_features: bfloat16 [32, 24, 8, 256], P('tm', 'grp'), parts along dimension 1, may hold values from -6 to 6
- cotangent: bfloat16 [32, 24, 8, 256], P('tm', 'grp'), parts along dimension 1, may hold values from -6 to 6
- encoder_weight: bfloat16 [6912, 256], replicated, may hold values from -0.078125 to 0.078125
- down_weight: bfloat16 [2048, 256], replicated, may hold values from -0.125 to 0.125
- coarse_weight: bfloat16 [768, 256], replicated, may hold values from -0.21875 to 0.21875
- up_weight: bfloat16 [256, 2048], replicated, may hold values from -0.375 to 0.375
- decoder_weight: bfloat16 [6912, 256], replicated, may hold values from -0.078125 to 0.078125
- levels: int32 [256], replicated, may hold values from 3 to 8
Outputs:
- video_grad: bfloat16 [32, 24, 8, 256], P('tm', 'grp'), parts along dimension 1
- latent_codes: bfloat16 [16, 12, 4, 256], P('tm', 'grp'), parts along dimension 1
- down_grad: float32 [4096, 256], P(('grp', 'tm')), parts along dimension 0
- coarse_grad: float32 [1536, 256], P(('grp', 'tm')), parts along dimension 0
- up_grad: float32 [512, 2048], P(('grp', 'tm')), parts along dimension 0
There are 2 independent parts, one for each index of `grp`. A program takes and returns all parts, laid end to end along the dimension named above; an argument that names none is the same for every part. Nothing has to cross between parts.
All inputs are finite; a program needn't handle non-finite values.
Results may differ from a plain program's by a relative error of at most 0.018.
The roundings to bfloat16 on the way count: a program that leaves them out, or rounds other values in their place, can miss the bound.
Values may be sent and summed in bfloat16 or wider, within the bound.
A program may use at most 64 MiB of HBM per device.

v0:
```python
import math

import jax
import jax.numpy as jnp
from jax import lax
from jax.sharding import PartitionSpec as P

two_pi = 2.0 * math.pi


def from_behind(value, axis, steps):
    count = lax.axis_size(axis)
    leading, last = (max(0, -steps), min(count, count - steps))
    return lax.ppermute(value, axis, [(source, source + steps) for source in range(leading, last)])


def tap_rows(padded, frames, tile_rows, tile_cols):
    pieces = [
        padded[step_t : step_t + frames, step_r : step_r + tile_rows, step_c : step_c + tile_cols]
        for step_t in range(3)
        for step_r in range(3)
        for step_c in range(3)
    ]
    return jnp.concatenate(pieces, axis=-1).reshape(frames * tile_rows * tile_cols, -1)


def flip_taps(weight, count):
    channels = weight.shape[1]
    blocks = weight.reshape(count, channels, channels)[::-1]
    return jnp.transpose(blocks, (0, 2, 1)).reshape(count * channels, channels)


def to_depth(field):
    frames, tile_rows, tile_cols, channels = field.shape
    split = field.reshape(frames // 2, 2, tile_rows // 2, 2, tile_cols // 2, 2, channels)
    return jnp.transpose(split, (0, 2, 4, 1, 3, 5, 6)).reshape(
        frames // 2, tile_rows // 2, tile_cols // 2, 8 * channels
    )


def from_depth(field):
    frames, tile_rows, tile_cols, packed = field.shape
    channels = packed // 8
    split = field.reshape(frames, tile_rows, tile_cols, 2, 2, 2, channels)
    return jnp.transpose(split, (0, 3, 1, 4, 2, 5, 6)).reshape(
        2 * frames, 2 * tile_rows, 2 * tile_cols, channels
    )


def transposed_product(left, right):
    return lax.dot_general(
        left, right, (((0,), (0,)), ((), ())), preferred_element_type=jnp.float32
    )


def product_with_transpose(left, right):
    return lax.dot_general(
        left, right, (((1,), (1,)), ((), ())), preferred_element_type=jnp.float32
    )


def time_columns(padded, frames):
    channels = padded.shape[-1]
    pieces = [padded[step_t : step_t + frames] for step_t in range(3)]
    return jnp.concatenate(pieces, axis=-1).reshape(-1, 3 * channels)


def spatial_pad(field):
    return jnp.pad(field, ((0, 0), (1, 1), (1, 1), (0, 0)))


def fine_patches(field):
    frames, tile_rows, tile_cols, channels = field.shape
    earlier = from_behind(field, "tm", 1)
    joined = jnp.concatenate([earlier, field], axis=0)
    return tap_rows(spatial_pad(joined), frames, tile_rows, tile_cols)


def fine_future(grad_field, weight):
    frames, tile_rows, tile_cols, channels = grad_field.shape
    later_frames = from_behind(grad_field, "tm", -1)
    joined = jnp.concatenate([grad_field, later_frames], axis=0)
    patches = tap_rows(spatial_pad(joined), frames, tile_rows, tile_cols)
    return jnp.dot(patches, flip_taps(weight, 27), preferred_element_type=jnp.float32).reshape(
        grad_field.shape
    )


def quantize(padded, frames, coarse_weight, half_range):
    columns = time_columns(padded, frames)
    pre_code = jnp.dot(columns, coarse_weight, preferred_element_type=jnp.float32)
    squashed = jnp.tanh(pre_code)
    bounded = half_range * squashed
    code_values = ((bounded - jnp.sin(two_pi * bounded) / two_pi) / half_range).astype(jnp.bfloat16)
    return (code_values, (columns, squashed, bounded))


def code_backward(code_grad, state):
    columns, squashed, bounded = state
    factor = (1.0 - jnp.cos(two_pi * bounded)) * (1.0 - squashed * squashed)
    return (code_grad.astype(jnp.float32) * factor).astype(jnp.bfloat16)


def coarse_earlier(latent):
    frames = latent.shape[0]
    shift_count = (frames + 1) // frames
    pieces = [from_behind(latent, "tm", lag_dev) for lag_dev in range(shift_count, 0, -1)]
    joined = jnp.concatenate(pieces + [latent], axis=0)
    return joined


def coarse_later(field):
    frames = field.shape[0]
    shift_count = (frames + 1) // frames
    pieces = [from_behind(field, "tm", -lag_dev) for lag_dev in range(1, shift_count + 1)]
    joined = jnp.concatenate([field] + pieces, axis=0)
    return joined


def spread_forward(latent, coarse_weight, half_range):
    code_values, state = quantize(
        coarse_earlier(latent), latent.shape[0], coarse_weight, half_range
    )
    return (code_values.reshape(latent.shape), state)


def spread_backward(code_field, state, coarse_weight):
    frames = code_field.shape[0]
    channels = code_field.shape[-1]
    pre_grad = code_backward(code_field.reshape(-1, channels), state)
    later_cols = time_columns(coarse_later(pre_grad.reshape(code_field.shape)), frames)
    latent_grad = jnp.dot(
        later_cols, flip_taps(coarse_weight, 3), preferred_element_type=jnp.float32
    ).astype(jnp.bfloat16)
    return (latent_grad.reshape(code_field.shape), pre_grad)


def shards(
    video_features,
    cotangent,
    encoder_weight,
    down_weight,
    coarse_weight,
    up_weight,
    decoder_weight,
    levels,
):
    frames, tile_rows, tile_cols, channels = video_features.shape
    grad_scale = 1.0 / math.sqrt(frames * lax.axis_size("tm") * tile_rows * tile_cols)
    half_range = (levels.astype(jnp.float32) - 1.0) * 0.5
    enc_patches = fine_patches(video_features)
    pre_enc = jnp.dot(enc_patches, encoder_weight, preferred_element_type=jnp.float32).reshape(
        video_features.shape
    )
    hidden = (video_features.astype(jnp.float32) + jax.nn.silu(pre_enc)).astype(jnp.bfloat16)
    stacked = to_depth(hidden)
    packed_shape = stacked.shape
    coarse_shape = packed_shape[:3] + (channels,)
    stacked_rows = stacked.reshape(-1, 8 * channels)
    latent = (
        jnp.dot(stacked_rows, down_weight, preferred_element_type=jnp.float32)
        .astype(jnp.bfloat16)
        .reshape(coarse_shape)
    )
    latent_codes, coarse_state = spread_forward(latent, coarse_weight, half_range)
    code_rows = latent_codes.reshape(-1, channels)
    back_dec = fine_future(cotangent, decoder_weight)
    decoded_grad = (cotangent.astype(jnp.float32) + back_dec).astype(jnp.bfloat16)
    depth_grad = to_depth(decoded_grad).reshape(-1, 8 * channels)
    code_grad = product_with_transpose(depth_grad, up_weight).astype(jnp.bfloat16)
    code_field = code_grad.reshape(coarse_shape)
    latent_grad, pre_grad = spread_backward(code_field, coarse_state, coarse_weight)
    latent_rows = latent_grad.reshape(-1, channels)
    hidden_grad = from_depth(product_with_transpose(latent_rows, down_weight).reshape(packed_shape))
    sigmoid_pre = jax.nn.sigmoid(pre_enc)
    enc_pre_grad = (hidden_grad * sigmoid_pre * (1.0 + pre_enc * (1.0 - sigmoid_pre))).astype(
        jnp.bfloat16
    )
    back_enc = fine_future(enc_pre_grad, encoder_weight)
    video_grad = (hidden_grad + back_enc).astype(jnp.bfloat16)
    count = lax.axis_size("tm")

    def slices(rows):
        return rows.reshape(rows.shape[0], count, -1).transpose(1, 0, 2)

    left = jnp.concatenate(
        [slices(stacked_rows), slices(coarse_state[0]), slices(code_rows)], axis=-1
    )
    left = lax.all_to_all(left, "tm", 0, 0, tiled=True)
    left = left.reshape(-1, left.shape[-1])
    right = lax.all_gather(jnp.concatenate([latent_rows, pre_grad], axis=-1), "tm", tiled=True)
    depth_all = lax.all_gather(depth_grad, "tm", tiled=True)
    down_cols = stacked_rows.shape[1] // count
    coarse_cols = coarse_state[0].shape[1] // count
    down_grad = transposed_product(left[:, :down_cols], right[:, :channels]) * grad_scale
    coarse_grad = (
        transposed_product(left[:, down_cols : down_cols + coarse_cols], right[:, channels:])
        * grad_scale
    )
    up_grad = transposed_product(left[:, down_cols + coarse_cols :], depth_all) * grad_scale
    return (video_grad, latent_codes, down_grad, coarse_grad, up_grad)


def solution(mesh):
    placed = (P("tm", "grp", None, None), P("tm", "grp", None, None), P(), P(), P(), P(), P(), P())
    return jax.shard_map(
        shards,
        mesh=mesh,
        in_specs=placed,
        out_specs=(
            P("tm", "grp", None, None),
            P("tm", "grp", None, None),
            P(("grp", "tm"), None),
            P(("grp", "tm"), None),
            P(("grp", "tm"), None),
        ),
        check_vma=False,
    )
```

profile of v0, /device:TPU:0, one launch (start us, length us, event | category | flops | bytes accessed | tf_op | source)
XLA Modules:
  0.0 104.6 jit_solution(12740343813124322159)
XLA Ops:
  7.2 0.0 copy-start
  7.2 0.0 all-gather.2.cloned.1.call-start
  7.2 1.4 %collective-permute-start = (bf16[2,12,8,256]{3,2,1,0:T(8,128)(2,1)}, bf16[2,12,8,256]{3,2,1,0:T(8,128)(2,1)S(1)}, u32[]{:S(2)}, u32[]{:S(2)}) collective-permute-start(bf16[2,12,8,256]{3,2,1,0:T(8,128)(2,1)} %param.9), channel_id=1, source_target_pairs={{1,0},{2,1},{3,2},{4,3},{5,4},{6,5},{7,6},{8,7},{9,8},{10,9},{11,1... | collective-permute-start | bytes 294920 | tf_op jit(solution)/shard_map/ppermute | solution.py:14
  8.7 3.0 %collective-permute-start.1 = (bf16[2,12,8,256]{3,2,1,0:T(8,128)(2,1)}, bf16[2,12,8,256]{3,2,1,0:T(8,128)(2,1)S(1)}, u32[]{:S(2)}, u32[]{:S(2)}) collective-permute-start(bf16[2,12,8,256]{3,2,1,0:T(8,128)(2,1)} %param.8), channel_id=1, source_target_pairs={{0,1},{1,2},{2,3},{3,4},{4,5},{5,6},{6,7},{7,8},{8,9},{9,10},{10,1... | collective-permute-start | bytes 294920 | tf_op jit(solution)/shard_map/ppermute | solution.py:14
  11.7 1.0 reverse_bitcast_fusion.2
  12.7 0.2 copy.32
  12.9 4.2 %reverse_bitcast_fusion.1 = bf16[27,256,256]{1,2,0:T(8,128)(2,1)} fusion(bf16[27,256,256]{2,1,0:T(8,128)(2,1)} %bitcast.59), kind=kLoop, calls=%fused_computation.3 | loop fusion | bytes 7077888 | tf_op jit(solution)/shard_map/transpose | solution.py:30
  17.1 5.7 %copy.29 = bf16[27,256,256]{2,1,0:T(8,128)(2,1)} copy(bf16[27,256,256]{1,2,0:T(8,128)(2,1)} %reverse_bitcast_fusion.1) | data formatting | bytes 7077888 | tf_op jit(solution)/shard_map/transpose | solution.py:30
  22.8 4.2 %reverse_bitcast_fusion = bf16[27,256,256]{1,2,0:T(8,128)(2,1)} fusion(bf16[27,256,256]{2,1,0:T(8,128)(2,1)} %bitcast.60), kind=kLoop, calls=%fused_computation.2 | loop fusion | bytes 7077888 | tf_op jit(solution)/shard_map/transpose | solution.py:30
  27.1 5.8 %copy.34 = bf16[27,256,256]{2,1,0:T(8,128)(2,1)} copy(bf16[27,256,256]{1,2,0:T(8,128)(2,1)} %reverse_bitcast_fusion) | data formatting | bytes 7077888 | tf_op jit(solution)/shard_map/transpose | solution.py:30
  33.1 0.0 copy-start.2
  33.7 1.5 %copy-done.2 = bf16[6912,256]{1,0:T(8,128)(2,1)S(1)} copy-done((bf16[6912,256]{1,0:T(8,128)(2,1)S(1)}, bf16[6912,256]{1,0:T(8,128)(2,1)}, u32[]{:S(2)}) %copy-start.2) | copy-done | bytes 3538968
  35.1 0.9 add_convert_fusion
  36.1 0.1 copy.43
  36.2 0.3 convolution_convert_fusion
  36.5 4.5 %collective-permute-start.3 = (bf16[1,6,4,256]{3,2,1,0:T(4,128)(2,1)S(1)}, bf16[1,6,4,256]{3,2,1,0:T(4,128)(2,1)S(1)}, u32[]{:S(2)}, u32[]{:S(2)}) collective-permute-start(bf16[1,6,4,256]{3,2,1,0:T(4,128)(2,1)S(1)} %reshape.76), channel_id=1, source_target_pairs={{0,1},{1,2},{2,3},{3,4},{4,5},{5,6},{6,7},{7,8},{8,9},{9,10},{10,1... | collective-permute-start | bytes 36872 | tf_op jit(solution)/shard_map/ppermute | solution.py:14
  41.0 4.3 %collective-permute-start.2 = (bf16[1,6,4,256]{3,2,1,0:T(4,128)(2,1)S(1)}, bf16[1,6,4,256]{3,2,1,0:T(4,128)(2,1)S(1)}, u32[]{:S(2)}, u32[]{:S(2)}) collective-permute-start(bf16[1,6,4,256]{3,2,1,0:T(4,128)(2,1)S(1)} %reshape.76), channel_id=1, source_target_pairs={{0,2},{1,3},{2,4},{3,5},{4,6},{5,7},{6,8},{7,9},{8,10},{9,11},{10,... | collective-permute-start | bytes 36872 | tf_op jit(solution)/shard_map/ppermute | solution.py:14
  45.3 0.0 collective-permute-done
  46.1 1.5 %copy-done.3 = bf16[27,256,256]{2,1,0:T(8,128)(2,1)S(1)} copy-done((bf16[27,256,256]{2,1,0:T(8,128)(2,1)S(1)}, bf16[27,256,256]{2,1,0:T(8,128)(2,1)}, u32[]{:S(2)}) %copy-start.3) | copy-done | bytes 3538968
  47.6 0.9 fusion.2
  48.4 0.1 reshape_reshape_reshape.6
  48.5 0.1 copy.44
  48.6 0.7 reshape_reshape.12
  49.3 0.0 all-gather.2.cloned.1.call-update
  49.4 0.0 collective-permute-done.2
  49.4 0.3 divide_convert_fusion
  49.7 1.3 %fusion.6 = bf16[24,256]{1,0:T(8,128)(2,1)S(1)} fusion(bf16[24,2048]{1,0:T(8,128)(2,1)} %reshape_reshape.12, bf16[256,2048]{1,0:T(8,128)(2,1)S(1)} %copy-done.5, f32[24,256]{1,0:T(8,128)S(1)} %get-tuple-element.8, f32[256]{0:T(256)S(1)} %add_multiply_fusion), kind=kOutput, calls=%fused_computation.88 | convolution fusion | flops 25227264 | bytes 1184768 | tf_op jit(solution)/shard_map/dot_general | solution.py:57
  51.0 1.3 %collective-permute-start.5 = (bf16[1,6,4,256]{3,2,1,0:T(4,128)(2,1)S(1)}, bf16[1,6,4,256]{3,2,1,0:T(4,128)(2,1)S(1)}, u32[]{:S(2)}, u32[]{:S(2)}) collective-permute-start(bf16[1,6,4,256]{3,2,1,0:T(4,128)(2,1)S(1)} %reshape.77), channel_id=1, source_target_pairs={{2,0},{3,1},{4,2},{5,3},{6,4},{7,5},{8,6},{9,7},{10,8},{11,9},{12,... | collective-permute-start | bytes 36872 | tf_op jit(solution)/shard_map/ppermute | solution.py:14
  52.3 1.3 %collective-permute-start.4 = (bf16[1,6,4,256]{3,2,1,0:T(4,128)(2,1)S(1)}, bf16[1,6,4,256]{3,2,1,0:T(4,128)(2,1)S(1)}, u32[]{:S(2)}, u32[]{:S(2)}) collective-permute-start(bf16[1,6,4,256]{3,2,1,0:T(4,128)(2,1)S(1)} %reshape.77), channel_id=1, source_target_pairs={{1,0},{2,1},{3,2},{4,3},{5,4},{6,5},{7,6},{8,7},{9,8},{10,9},{11,1... | collective-permute-start | bytes 36872 | tf_op jit(solution)/shard_map/ppermute | solution.py:14
  53.6 0.1 reshape_reshape_reshape.7
  53.8 0.1 reshape_reshape.15
  53.9 0.1 pad_maximum_fusion.1
  54.0 0.6 reshape.83
  54.6 0.7 copy.35
  55.4 7.8 %all-to-all-start = ((bf16[16,24,192]{2,1,0:T(8,128)(2,1)}), bf16[16,24,192]{2,1,0:T(8,128)(2,1)S(1)}, u32[]{:S(2)}, u32[]{:S(2)}) async-start(bf16[16,24,192]{2,1,0:T(8,128)(2,1)} %copy.35), calls=%async_computation | async-start | bytes 393216 | tf_op jit(solution)/shard_map/all_to_all | solution.py:189
  63.2 0.1 convolution_convert_fusion.2
  63.4 0.4 fusion.25
  63.8 0.2 reshape_reshape.14
  64.0 0.1 reshape.80
  64.2 0.1 multiply_convert_fusion
  64.2 1.3 %collective-permute-start.6 = (bf16[2,12,8,256]{3,2,1,0:T(8,128)(2,1)S(1)}, bf16[2,12,8,256]{3,2,1,0:T(8,128)(2,1)S(1)}, u32[]{:S(2)}, u32[]{:S(2)}) collective-permute-start(bf16[2,12,8,256]{3,2,1,0:T(8,128)(2,1)S(1)} %multiply_convert_fusion), channel_id=1, source_target_pairs={{1,0},{2,1},{3,2},{4,3},{5,4},{6,5},{7,6},{8,7},{9,8},{10,9},{11,1... | collective-permute-start | bytes 294920 | tf_op jit(solution)/shard_map/ppermute | solution.py:14
  65.5 24.2 %all_gather.6 = bf16[384,512]{1,0:T(8,128)(2,1)S(1)} all-gather(bf16[24,512]{1,0:T(8,128)(2,1)S(1)} %pad_maximum_fusion.3), channel_id=1, replica_groups=mesh['grp'=2,'tm'=16] {'tm'}, dimensions={0}, use_global_device_ids=true | all-gather | bytes 417792 | tf_op jit(solution)/shard_map/all_gather | solution.py:191
  89.8 0.0 collective-permute-done.6
  90.5 1.5 %copy-done.1 = bf16[27,256,256]{2,1,0:T(8,128)(2,1)S(1)} copy-done((bf16[27,256,256]{2,1,0:T(8,128)(2,1)S(1)}, bf16[27,256,256]{2,1,0:T(8,128)(2,1)}, u32[]{:S(2)}) %copy-start.1) | copy-done | bytes 3538968
  92.0 1.5 %fusion.3 = bf16[2,12,8,256]{3,2,1,0:T(8,128)(2,1)} fusion(f32[2,12,8,256]{3,2,1,0:T(8,128)S(1)} %reshape.80, bf16[2,12,8,6912]{3,2,1,0:T(8,128)(2,1)S(1)} %constant_dynamic-update-slice_fusion.58, bf16[6912,256,1,1]{1,0,3,2:T(8,128)(2,1)S(1)} %bitcast.58), kind=kOutput, calls=%fused_computation.80 | convolution fusion | flops 679575552 | bytes 6488064 | tf_op jit(solution)/shard_map/dot_general | solution.py:84
  93.5 0.8 convolution_multiply_fusion.2
  94.3 0.9 convolution_multiply_fusion.1
  95.2 2.5 %convolution_multiply_fusion = f32[16,2048]{1,0:T(8,128)} fusion(bf16[384,2048]{1,0:T(8,128)(2,1)} %all-gather.2.cloned.1.call-done, bf16[384,192]{1,0:T(8,128)(2,1)S(1)} %bitcast.66), kind=kOutput, calls=%fused_computation.4 | convolution fusion | flops 25198592 | bytes 1802240 | tf_op jit(solution)/shard_map/dot_general | solution.py:51
  (118 shorter events, 2.0 us)
Async XLA Ops:
  7.2 29.1 %copy-start = (bf16[2048,256]{1,0:T(8,128)(2,1)S(1)}, bf16[2048,256]{1,0:T(8,128)(2,1)}, u32[]{:S(2)}) copy-start(bf16[2048,256]{1,0:T(8,128)(2,1)} %param.11) | copy-start | bytes 3145732
  7.2 88.1 %all-gather.2.cloned.1.call-start = ((), (), s32[]{:S(2)}) async-start(), calls=%async_computation.1 | async-start | bytes 1671168 | tf_op jit(solution)/shard_map/all_gather | solution.py:192
  7.2 38.1 %collective-permute-start = (bf16[2,12,8,256]{3,2,1,0:T(8,128)(2,1)}, bf16[2,12,8,256]{3,2,1,0:T(8,128)(2,1)S(1)}, u32[]{:S(2)}, u32[]{:S(2)}) collective-permute-start(bf16[2,12,8,256]{3,2,1,0:T(8,128)(2,1)} %param.9), channel_id=1, source_target_pairs={{1,0},{2,1},{3,2},{4,3},{5,4},{6,5},{7,6},{8,7},{9,8},{10,9},{11,1... | collective-permute-start | bytes 294920 | tf_op jit(solution)/shard_map/ppermute | solution.py:14
  8.7 24.2 %collective-permute-start.1 = (bf16[2,12,8,256]{3,2,1,0:T(8,128)(2,1)}, bf16[2,12,8,256]{3,2,1,0:T(8,128)(2,1)S(1)}, u32[]{:S(2)}, u32[]{:S(2)}) collective-permute-start(bf16[2,12,8,256]{3,2,1,0:T(8,128)(2,1)} %param.8), channel_id=1, source_target_pairs={{0,1},{1,2},{2,3},{3,4},{4,5},{5,6},{6,7},{7,8},{8,9},{9,10},{10,1... | collective-permute-start | bytes 294920 | tf_op jit(solution)/shard_map/ppermute | solution.py:14
  17.1 5.7 %copy-start.8 = (s32[256]{0:T(256)S(1)}, s32[256]{0:T(256)}, u32[]{:S(2)}) copy-start(s32[256]{0:T(256)} %param.15) | copy-start | bytes 3076
  27.1 5.8 %copy-start.7 = (bf16[2,12,8,256]{3,2,1,0:T(8,128)(2,1)S(1)}, bf16[2,12,8,256]{3,2,1,0:T(8,128)(2,1)}, u32[]{:S(2)}) copy-start(bf16[2,12,8,256]{3,2,1,0:T(8,128)(2,1)} %param.9) | copy-start | bytes 294916
  27.1 5.8 %copy-start.6 = (bf16[2,12,8,256]{3,2,1,0:T(8,128)(2,1)S(1)}, bf16[2,12,8,256]{3,2,1,0:T(8,128)(2,1)}, u32[]{:S(2)}) copy-start(bf16[2,12,8,256]{3,2,1,0:T(8,128)(2,1)} %param.8) | copy-start | bytes 294916
  33.1 2.0 %copy-start.2 = (bf16[6912,256]{1,0:T(8,128)(2,1)S(1)}, bf16[6912,256]{1,0:T(8,128)(2,1)}, u32[]{:S(2)}) copy-start(bf16[6912,256]{1,0:T(8,128)(2,1)} %param.10) | copy-start | bytes 10616836
  36.5 12.8 %collective-permute-start.3 = (bf16[1,6,4,256]{3,2,1,0:T(4,128)(2,1)S(1)}, bf16[1,6,4,256]{3,2,1,0:T(4,128)(2,1)S(1)}, u32[]{:S(2)}, u32[]{:S(2)}) collective-permute-start(bf16[1,6,4,256]{3,2,1,0:T(4,128)(2,1)S(1)} %reshape.76), channel_id=1, source_target_pairs={{0,1},{1,2},{2,3},{3,4},{4,5},{5,6},{6,7},{7,8},{8,9},{9,10},{10,1... | collective-permute-start | bytes 36872 | tf_op jit(solution)/shard_map/ppermute | solution.py:14
  41.0 8.3 %collective-permute-start.2 = (bf16[1,6,4,256]{3,2,1,0:T(4,128)(2,1)S(1)}, bf16[1,6,4,256]{3,2,1,0:T(4,128)(2,1)S(1)}, u32[]{:S(2)}, u32[]{:S(2)}) collective-permute-start(bf16[1,6,4,256]{3,2,1,0:T(4,128)(2,1)S(1)} %reshape.76), channel_id=1, source_target_pairs={{0,2},{1,3},{2,4},{3,5},{4,6},{5,7},{6,8},{7,9},{8,10},{9,11},{10,... | collective-permute-start | bytes 36872 | tf_op jit(solution)/shard_map/ppermute | solution.py:14
  45.6 2.0 %copy-start.3 = (bf16[27,256,256]{2,1,0:T(8,128)(2,1)S(1)}, bf16[27,256,256]{2,1,0:T(8,128)(2,1)}, u32[]{:S(2)}) copy-start(bf16[27,256,256]{2,1,0:T(8,128)(2,1)} %copy.29) | copy-start | bytes 10616836
  47.6 1.8 %copy-start.4 = (bf16[768,256]{1,0:T(8,128)(2,1)S(1)}, bf16[768,256]{1,0:T(8,128)(2,1)}, u32[]{:S(2)}) copy-start(bf16[768,256]{1,0:T(8,128)(2,1)} %param.12) | copy-start | bytes 1179652
  47.6 2.1 %copy-start.5 = (bf16[256,2048]{1,0:T(8,128)(2,1)S(1)}, bf16[256,2048]{1,0:T(8,128)(2,1)}, u32[]{:S(2)}) copy-start(bf16[256,2048]{1,0:T(8,128)(2,1)} %param.13) | copy-start | bytes 3145732
  51.0 12.1 %collective-permute-start.5 = (bf16[1,6,4,256]{3,2,1,0:T(4,128)(2,1)S(1)}, bf16[1,6,4,256]{3,2,1,0:T(4,128)(2,1)S(1)}, u32[]{:S(2)}, u32[]{:S(2)}) collective-permute-start(bf16[1,6,4,256]{3,2,1,0:T(4,128)(2,1)S(1)} %reshape.77), channel_id=1, source_target_pairs={{2,0},{3,1},{4,2},{5,3},{6,4},{7,5},{8,6},{9,7},{10,8},{11,9},{12,... | collective-permute-start | bytes 36872 | tf_op jit(solution)/shard_map/ppermute | solution.py:14
  52.3 10.9 %collective-permute-start.4 = (bf16[1,6,4,256]{3,2,1,0:T(4,128)(2,1)S(1)}, bf16[1,6,4,256]{3,2,1,0:T(4,128)(2,1)S(1)}, u32[]{:S(2)}, u32[]{:S(2)}) collective-permute-start(bf16[1,6,4,256]{3,2,1,0:T(4,128)(2,1)S(1)} %reshape.77), channel_id=1, source_target_pairs={{1,0},{2,1},{3,2},{4,3},{5,4},{6,5},{7,6},{8,7},{9,8},{10,9},{11,1... | collective-permute-start | bytes 36872 | tf_op jit(solution)/shard_map/ppermute | solution.py:14
  55.4 38.2 %all-to-all-start = ((bf16[16,24,192]{2,1,0:T(8,128)(2,1)}), bf16[16,24,192]{2,1,0:T(8,128)(2,1)S(1)}, u32[]{:S(2)}, u32[]{:S(2)}) async-start(bf16[16,24,192]{2,1,0:T(8,128)(2,1)} %copy.35), calls=%async_computation | async-start | bytes 393216 | tf_op jit(solution)/shard_map/all_to_all | solution.py:189
  64.2 25.5 %collective-permute-start.6 = (bf16[2,12,8,256]{3,2,1,0:T(8,128)(2,1)S(1)}, bf16[2,12,8,256]{3,2,1,0:T(8,128)(2,1)S(1)}, u32[]{:S(2)}, u32[]{:S(2)}) collective-permute-start(bf16[2,12,8,256]{3,2,1,0:T(8,128)(2,1)S(1)} %multiply_convert_fusion), channel_id=1, source_target_pairs={{1,0},{2,1},{3,2},{4,3},{5,4},{6,5},{7,6},{8,7},{9,8},{10,9},{11,1... | collective-permute-start | bytes 294920 | tf_op jit(solution)/shard_map/ppermute | solution.py:14
  90.0 2.0 %copy-start.1 = (bf16[27,256,256]{2,1,0:T(8,128)(2,1)S(1)}, bf16[27,256,256]{2,1,0:T(8,128)(2,1)}, u32[]{:S(2)}) copy-start(bf16[27,256,256]{2,1,0:T(8,128)(2,1)} %copy.34) | copy-start | bytes 10616836
Sparse Core Ops, SparseCore 0:
  49.5 41.1 all-gather.1
where the time goes:
time: 105 us
  local copies, waits for them, and re-layouts  30.3 us (29%)
  starting transfers between devices  24.9 us (24%)
  blocking collectives  24.2 us (23%)
  between operations  15 us (14%)
  matrix products  9.81 us (9%)
    all_gather x1, blocking collectives, shards(): lax.all_gather(jnp.concatenate([latent_rows, pre_grad], axis=-1), 'tm', t...  24.2 us
    transpose x6, local copies, waits for them, and re-layouts, flip_taps(): return jnp.transpose(blocks, (0, 2, 1)).reshape(count * channels, channels)  21.1 us
    ppermute x7, starting transfers between devices, from_behind(): lax.ppermute(value, axis, [(source, source + steps) for source in range(l...  17.1 us
    all_to_all x1, starting transfers between devices, shards(): left = lax.all_to_all(left, 'tm', 0, 0, tiled=True)  7.79 us
    unnamed x97, local copies, waits for them, and re-layouts  6.02 us
    dot_general x3, matrix products, transposed_product(): lax.dot_general(left, right, (((0,), (0,)), ((), ())), preferred_element_...  4.18 us
    dot_general x2, matrix products, fine_future(): jnp.dot(patches, flip_taps(weight, 27), preferred_element_type=jnp.float32)  2.35 us
  transfers between devices with their start and end apart: 9, of which 0 were waited for; matrix products, arithmetic and copies ran while one was open for 32% of the time, Pallas kernels for 0%

commit v1 on v0

v1 whole, which is shorter than its diff:
```python
import functools
import math

import jax
import jax.numpy as jnp
import numpy as np
from jax import lax
from jax.experimental import pallas as pl
from jax.experimental.pallas import tpu as pltpu
from jax.sharding import PartitionSpec as P

two_pi = 2.0 * math.pi
BF = jnp.bfloat16
F32 = jnp.float32
MESH = pl.DeviceIdType.MESH

HALO_V, HALO_C, HALO_E = 0, 1, 2
LAT, PRE, COD, LGR, COLS, UPS = 0, 1, 2, 3, 4, 5


def mm(a, b):
    return jnp.dot(a, b, preferred_element_type=F32)


def mm_nt(a, b):
    return lax.dot_general(a, b, (((1,), (1,)), ((), ())), preferred_element_type=F32)


def mm_tn(a, b):
    return lax.dot_general(a, b, (((0,), (0,)), ((), ())), preferred_element_type=F32)


def depth_permutation(rows, cols):
    order = np.arange(2 * rows * cols).reshape(2, rows // 2, 2, cols // 2, 2)
    order = order.transpose(0, 2, 4, 1, 3).reshape(-1)
    picks = np.zeros((order.size, order.size), np.float32)
    picks[np.arange(order.size), order] = 1.0
    return picks


def kernel(
    n, scale, vf, ct, we, wd, wc, wu, wx, half, perm,
    vg_out, code_out, down_out, coarse_out, up_out,
    vbuf, cbuf, ebuf, we_v, wx_v, wd_v, wc_v, wu_v, perm_v, half_v,
    lat, pre, cod, lgr, cols_mine, cols_all, up_mine, up_all,
    vg_v, code_v, down_v, coarse_v, up_v, coarse_cut, up_cut,
    hal_s, hal_r, msg_s, msg_r, load_sem, out_sem,
):
    frames, rows, width, ch = vf.shape
    fine = frames * rows * width
    cells = fine // 8
    deep = wd.shape[0]
    nb, _, _, wb = cols_mine.shape
    rep = n // nb
    me = lax.axis_index("tm")

    def peer_of(k):
        return lax.rem(me + k, n)

    barrier = pltpu.get_barrier_semaphore()

    @pl.loop(1, n)
    def _(k):
        pl.semaphore_signal(barrier, inc=1, device_id={"tm": peer_of(k)}, device_id_type=MESH)

    third = we.shape[0] // 3
    loads = [
        pltpu.make_async_copy(vf, vbuf.at[2:4, 1 : rows + 1], load_sem.at[0]),
        pltpu.make_async_copy(ct, cbuf.at[0:2, 1 : rows + 1], load_sem.at[1]),
    ]
    for k, part in enumerate((2, 1, 0)):
        span = pl.ds(part * third, third)
        loads.append(pltpu.make_async_copy(we.at[span], we_v.at[span], load_sem.at[2 + k]))
        loads.append(pltpu.make_async_copy(wx.at[span], wx_v.at[span], load_sem.at[5 + k]))
    small = [
        pltpu.make_async_copy(src, dst, load_sem.at[8 + k])
        for k, (src, dst) in enumerate(
            ((perm, perm_v), (wd, wd_v), (wu, wu_v), (wc, wc_v), (half, half_v))
        )
    ]
    for load in loads[:4] + loads[4:] + small:
        load.start()

    def halo(kind, src, dst, peer):
        return pltpu.make_async_remote_copy(
            src_ref=src, dst_ref=dst, send_sem=hal_s.at[kind], recv_sem=hal_r.at[kind],
            device_id={"tm": peer}, device_id_type=MESH,
        )

    def message(kind, src, dst, peer, source):
        return pltpu.make_async_remote_copy(
            src_ref=src, dst_ref=dst, send_sem=msg_s.at[kind, peer], recv_sem=msg_r.at[kind, source],
            device_id={"tm": peer}, device_id_type=MESH,
        )

    first, last = me == 0, me == n - 1
    inner = pl.ds(1, rows)

    def rows_out(buf, at, out, cut, sem):
        count = out.shape[0]
        if count % 8 == 0:
            return pltpu.make_async_copy(buf.at[pl.ds(pl.multiple_of(at, 8), count)], out, sem)
        for k in range(count):
            cut[pl.ds(k, 1)] = buf[pl.ds(at + k, 1)]
        return pltpu.make_async_copy(cut, out, sem)

    def send_v():
        return halo(HALO_V, vf, vbuf.at[0:2, inner], me + 1)

    def send_c():
        return halo(HALO_C, ct, cbuf.at[2:4, inner], me - 1)

    def send_e():
        return halo(HALO_E, ebuf.at[0:2, inner], ebuf.at[2:4, inner], me - 1)

    edge = jnp.zeros((4, 1, width, ch), BF)
    for buf in (vbuf, cbuf, ebuf):
        buf[:, 0:1] = edge
        buf[:, rows + 1 : rows + 2] = edge
    blank = jnp.zeros((2, rows, width, ch), BF)

    @pl.when(first)
    def _():
        vbuf[0:2, 1 : rows + 1] = blank

    @pl.when(last)
    def _():
        cbuf[2:4, 1 : rows + 1] = blank
        ebuf[2:4, 1 : rows + 1] = blank

    lat[0:2] = jnp.zeros((2, cells, ch), BF)
    pre[n : n + 2] = jnp.zeros((2, cells, ch), BF)

    pl.semaphore_wait(barrier, n - 1)

    @pl.when(me < n - 1)
    def _():
        send_v().start()

    @pl.when(me > 0)
    def _():
        send_c().start()

    def taps(buf, p):
        return [buf[p : p + 2, q : q + rows].reshape(fine, ch) for q in range(3)]

    def past(buf, weight, p):
        left = jnp.concatenate(taps(buf, p), axis=1)
        out = []
        for r in range(3):
            right = jnp.concatenate(
                [weight[pl.ds(((3 * p + q) * 3 + r) * ch, ch)] for q in range(3)], axis=0
            )
            out.append(mm(left, right))
        return out

    def future(buf, weight, p):
        left = jnp.concatenate(taps(buf, p), axis=1)
        out = []
        for r in range(3):
            right = jnp.concatenate(
                [
                    weight[pl.ds((((2 - p) * 3 + 2 - q) * 3 + 2 - r) * ch, ch)]
                    for q in range(3)
                ],
                axis=1,
            )
            out.append(mm_nt(left, right))
        return out

    def added(a, b):
        return [x + y for x, y in zip(a, b)]

    lane = lax.broadcasted_iota(jnp.int32, (fine // width, width, ch), 1)

    def aligned(parts):
        a, b, c = [x.reshape(fine // width, width, ch) for x in parts]
        a = jnp.where(lane == 0, 0.0, pltpu.roll(a, 1, 1))
        c = jnp.where(lane == width - 1, 0.0, pltpu.roll(c, width - 1, 1))
        return (a + b + c).reshape(fine, ch)

    loads[0].wait()
    loads[2].wait()
    enc = past(vbuf, we_v, 2)
    loads[1].wait()
    loads[3].wait()
    dec = future(cbuf, wx_v, 0)
    loads[4].wait()
    loads[6].wait()

    @pl.when(me > 0)
    def _():
        send_v().wait_recv()

    enc = added(enc, past(vbuf, we_v, 1))
    enc = added(enc, past(vbuf, we_v, 0))
    pre_enc = aligned(enc)
    sig = jax.nn.sigmoid(pre_enc)
    own = vbuf[2:4, 1 : rows + 1].reshape(fine, ch).astype(F32)
    hidden = (own + pre_enc * sig).astype(BF)
    slope = sig * (1.0 + pre_enc * (1.0 - sig))

    for load in small:
        load.wait()

    def regroup(field):
        moved = mm(perm_v[0], field)
        return [moved[b * cells : (b + 1) * cells].astype(BF) for b in range(8)]

    def keep_columns(slot, blocks):
        per = nb // 8
        for b in range(8):
            for h in range(per):
                cols_mine[b * per + h, slot] = blocks[b][:, h * wb : (h + 1) * wb]

    stacked = regroup(hidden)
    keep_columns(0, stacked)
    lat[me + 2] = mm(jnp.concatenate(stacked, axis=1), wd_v[...]).astype(BF)

    def gather(buf, kind, slot, peer):
        return message(kind, buf.at[slot], buf.at[slot], peer, me)

    @pl.loop(1, n)
    def _(k):
        gather(lat, LAT, me + 2, peer_of(k)).start()

    loads[5].wait()
    loads[7].wait()

    @pl.when(me < n - 1)
    def _():
        send_c().wait_recv()

    dec = added(dec, future(cbuf, wx_v, 1))
    dec = added(dec, future(cbuf, wx_v, 2))
    own_c = cbuf[0:2, 1 : rows + 1].reshape(fine, ch).astype(F32)
    depth = regroup((own_c + aligned(dec)).astype(BF))
    keep_columns(1, depth)
    code_grad = mm_nt(jnp.concatenate(depth, axis=1), wu_v[...]).astype(BF)

    def columns(peer):
        return message(COLS, cols_mine.at[peer // rep], cols_all.at[me], peer, me)

    for lag in (1, 2):
        @pl.when(me >= lag)
        def _():
            message(LAT, lat.at[me + 2], lat.at[me + 2 - lag], me, me - lag).wait_recv()

    frames_in = jnp.concatenate([lat[me + p] for p in range(3)], axis=1)
    squashed = jnp.tanh(mm(frames_in, wc_v[...]))
    half_range = half_v[...]
    bounded = half_range * squashed
    codes = ((bounded - jnp.sin(two_pi * bounded) / two_pi) / half_range).astype(BF)
    factor = (1.0 - jnp.cos(two_pi * bounded)) * (1.0 - squashed * squashed)
    pre[me] = (code_grad.astype(F32) * factor).astype(BF)

    @pl.loop(1, n)
    def _(k):
        gather(pre, PRE, me, peer_of(n - k)).start()

    cod[me] = codes
    code_v[...] = codes.reshape(code_v.shape)
    code_copy = pltpu.make_async_copy(code_v, code_out, out_sem.at[0])
    code_copy.start()

    @pl.loop(1, n)
    def _(k):
        columns(peer_of(k)).start()

    cols_all[me] = cols_mine[me // rep]

    @pl.loop(1, n)
    def _(k):
        gather(cod, COD, me, peer_of(k)).start()

    for lag in (1, 2):
        @pl.when(me < n - lag)
        def _():
            message(PRE, pre.at[me], pre.at[me + lag], me, me + lag).wait_recv()

    wc_flip = jnp.concatenate([wc_v[pl.ds((2 - p) * ch, ch)] for p in range(3)], axis=1)
    later = jnp.concatenate([pre[me + p] for p in range(3)], axis=1)
    grad_lat = mm_nt(later, wc_flip).astype(BF)
    lgr[me] = grad_lat

    deep_grad = mm_nt(grad_lat, wd_v[...])
    deep_rows = jnp.concatenate(
        [deep_grad[:, b * ch : (b + 1) * ch] for b in range(8)], axis=0
    )
    high = deep_rows.astype(BF)
    rest = deep_rows - high.astype(F32)
    middle = rest.astype(BF)
    low = (rest - middle.astype(F32)).astype(BF)
    back = perm_v[1]
    hidden_grad = mm(back, high) + (mm(back, middle) + mm(back, low))
    ebuf[0:2, 1 : rows + 1] = (hidden_grad * slope).astype(BF).reshape(2, rows, width, ch)

    @pl.when(me > 0)
    def _():
        send_e().start()

    @pl.loop(1, n)
    def _(k):
        gather(lgr, LGR, me, peer_of(k)).start()

    bck = future(ebuf, we_v, 0)

    @pl.loop(1, n)
    def _(k):
        source = peer_of(n - k)

        @pl.when((k > 2) | (source > me))
        def _():
            message(LAT, lat.at[me + 2], lat.at[source + 2], me, source).wait_recv()

    @pl.loop(1, n)
    def _(k):
        source = peer_of(k)

        @pl.when((k > 2) | (source < me))
        def _():
            message(PRE, pre.at[me], pre.at[source], me, source).wait_recv()

    @pl.loop(1, n)
    def _(k):
        source = peer_of(k)
        message(COLS, cols_mine.at[0], cols_all.at[source], me, source).wait_recv()

    @pl.loop(1, n)
    def _(k):
        source = peer_of(k)
        message(COD, cod.at[me], cod.at[source], me, source).wait_recv()

    total = n * cells
    up_part = mm_tn(cod[...].reshape(total, ch), cols_all[:, 1].reshape(total, wb)) * scale
    blocks, block_rows = up_mine.shape[0], up_mine.shape[1]
    up_mine[...] = up_part.reshape(blocks, block_rows, wb)
    up_rows = ch // n
    mine = lax.rem(me, rep)
    my_block = me // rep

    def up_target(k):
        return mine + rep * lax.rem(my_block + k, nb)

    def up_send(peer):
        return message(
            UPS, up_mine.at[peer * up_rows // block_rows], up_all.at[my_block], peer, me
        )

    @pl.loop(1, nb)
    def _(k):
        up_send(up_target(k)).start()

    up_all[my_block] = up_mine[me * up_rows // block_rows]

    pre_all = pre[0:n].reshape(total, ch)
    for p in range(3):
        coarse_v[pl.ds(p * ch, ch)] = mm_tn(lat[p : p + n].reshape(total, ch), pre_all) * scale
    coarse_copy = rows_out(coarse_v, me * coarse_out.shape[0], coarse_out, coarse_cut, out_sem.at[1])
    coarse_copy.start()

    @pl.when(me < n - 1)
    def _():
        send_e().wait_recv()

    bck = added(bck, future(ebuf, we_v, 1))
    bck = added(bck, future(ebuf, we_v, 2))
    vg_v[...] = (hidden_grad + aligned(bck)).astype(BF).reshape(vg_v.shape)
    vg_copy = pltpu.make_async_copy(vg_v, vg_out, out_sem.at[2])
    vg_copy.start()

    @pl.loop(1, n)
    def _(k):
        source = peer_of(k)
        message(LGR, lgr.at[me], lgr.at[source], me, source).wait_recv()

    down_v[...] = (
        mm_tn(cols_all[:, 0].reshape(total, wb), lgr[...].reshape(total, ch)) * scale
    )
    down_rows = down_out.shape[0]
    down_copy = rows_out(down_v, mine * down_rows, down_out, None, out_sem.at[3])
    down_copy.start()

    @pl.loop(1, nb)
    def _(k):
        source = up_target(k)
        message(UPS, up_mine.at[0], up_all.at[source // rep], me, source).wait_recv()

    for b in range(nb):
        up_v[:, b * wb : (b + 1) * wb] = up_all[b]
    up_copy = rows_out(up_v, lax.rem(me * up_rows, block_rows), up_out, up_cut, out_sem.at[4])
    up_copy.start()

    @pl.when(me < n - 1)
    def _():
        send_v().wait_send()

    @pl.when(me > 0)
    def _():
        send_c().wait_send()
        send_e().wait_send()

    @pl.loop(1, n)
    def _(k):
        peer = peer_of(k)
        gather(lat, LAT, me + 2, peer).wait_send()
        gather(pre, PRE, me, peer).wait_send()
        gather(cod, COD, me, peer).wait_send()
        gather(lgr, LGR, me, peer).wait_send()
        columns(peer).wait_send()

    @pl.loop(1, nb)
    def _(k):
        up_send(up_target(k)).wait_send()

    for copy in (code_copy, coarse_copy, vg_copy, down_copy, up_copy):
        copy.wait()


def shards(n, vf, ct, we, wd, wc, wu, wx, levels):
    frames, rows, width, ch = vf.shape
    deep = wd.shape[0]
    fine = frames * rows * width
    cells = fine // 8
    wb = max(128, deep // n)
    nb = deep // wb
    up_rows = ch // n
    block_rows = max(8, up_rows)
    scale = 1.0 / math.sqrt(n * fine)
    half = ((levels.astype(F32) - 1.0) * 0.5).reshape(1, ch)
    picks = depth_permutation(rows, width)
    perm = jnp.asarray(np.stack([picks, picks.T]), BF)
    anywhere = pl.BlockSpec(memory_space=pl.ANY)
    code_shape = (frames // 2, rows // 2, width // 2, ch)
    out_shape = (
        jax.ShapeDtypeStruct(vf.shape, BF),
        jax.ShapeDtypeStruct(code_shape, BF),
        jax.ShapeDtypeStruct((deep // n, ch), F32),
        jax.ShapeDtypeStruct((wc.shape[0] // n, ch), F32),
        jax.ShapeDtypeStruct((up_rows, deep), F32),
    )
    padded = (4, rows + 2, width, ch)
    scratch = [
        pltpu.VMEM(padded, BF), pltpu.VMEM(padded, BF), pltpu.VMEM(padded, BF),
        pltpu.VMEM(we.shape, BF), pltpu.VMEM(wx.shape, BF), pltpu.VMEM(wd.shape, BF),
        pltpu.VMEM(wc.shape, BF), pltpu.VMEM(wu.shape, BF), pltpu.VMEM(perm.shape, BF),
        pltpu.VMEM(half.shape, F32),
        pltpu.VMEM((n + 2, cells, ch), BF), pltpu.VMEM((n + 2, cells, ch), BF),
        pltpu.VMEM((n, cells, ch), BF), pltpu.VMEM((n, cells, ch), BF),
        pltpu.VMEM((nb, 2, cells, wb), BF), pltpu.VMEM((n, 2, cells, wb), BF),
        pltpu.VMEM((ch // block_rows, block_rows, wb), F32),
        pltpu.VMEM((nb, block_rows, wb), F32),
        pltpu.VMEM(vf.shape, BF), pltpu.VMEM(code_shape, BF), pltpu.VMEM((wb, ch), F32),
        pltpu.VMEM(wc.shape, F32), pltpu.VMEM((block_rows, deep), F32),
        pltpu.VMEM(out_shape[3].shape, F32), pltpu.VMEM(out_shape[4].shape, F32),
        pltpu.SemaphoreType.DMA((3,)), pltpu.SemaphoreType.DMA((3,)),
        pltpu.SemaphoreType.DMA((6, n)), pltpu.SemaphoreType.DMA((6, n)),
        pltpu.SemaphoreType.DMA((13,)), pltpu.SemaphoreType.DMA((5,)),
    ]
    return pl.pallas_call(
        functools.partial(kernel, n, scale),
        out_shape=out_shape,
        in_specs=[anywhere] * 9,
        out_specs=(anywhere,) * 5,
        scratch_shapes=scratch,
        compiler_params=pltpu.CompilerParams(collective_id=0, has_side_effects=True),
    )(vf, ct, we, wd, wc, wu, wx, half, perm)


def solution(mesh):
    placed = (P("tm", "grp", None, None), P("tm", "grp", None, None), P(), P(), P(), P(), P(), P())
    return jax.shard_map(
        functools.partial(shards, mesh.shape["tm"]),
        mesh=mesh,
        in_specs=placed,
        out_specs=(
            P("tm", "grp", None, None),
            P("tm", "grp", None, None),
            P(("grp", "tm"), None),
            P(("grp", "tm"), None),
            P(("grp", "tm"), None),
        ),
        check_vma=False,
    )
```

time: 105 us -> 48.1 us (0.46)
  Pallas kernels: 0 us -> 38.5 us
  starting transfers between devices: 24.9 us -> 0 us
  blocking collectives: 24.2 us -> 0 us
  local copies, waits for them, and re-layouts: 30.3 us -> 7.41 us
  between operations: 15 us -> 0.64 us
  matrix products: 9.81 us -> 0 us
    pallas_call x0 -> x1, Pallas kernels: none -> 38.5 us  [shards(): pl.pallas_call(functools.partial(kernel, n, scale), out_shape=out_shape,...]
    all_gather x1 -> x0, blocking collectives: 24.2 us -> none  [shards(): lax.all_gather(jnp.concatenate([latent_rows, pre_grad], axis=-1), 'tm', t...]
    transpose x6 -> x0, local copies, waits for them, and re-layouts: 21.1 us -> none  [flip_taps(): return jnp.transpose(blocks, (0, 2, 1)).reshape(count * channels, channels)]
    ppermute x7 -> x0, starting transfers between devices: 17.1 us -> none  [from_behind(): lax.ppermute(value, axis, [(source, source + steps) for source in range(l...]
    dot_general x11 -> x0, matrix products: 9.81 us -> none  [the longest x3 4.18 us: transposed_product(): lax.dot_general(left, right, (((0,), (0,)), ((), ())), preferred_element_...]
    all_to_all x1 -> x0, starting transfers between devices: 7.79 us -> none  [shards(): left = lax.all_to_all(left, 'tm', 0, 0, tiled=True)]
    unnamed x97 -> x5, local copies, waits for them, and re-layouts: 6.02 us -> 7.41 us
    another operation x7 -> x0, local copies, waits for them, and re-layouts: 1.28 us -> none  [the longest x1 0.69 us: shards(): depth_grad = to_depth(decoded_grad).reshape(-1, 8 * channels)]
  transfers between devices with their start and end apart: 9 -> 0, of which waited for: 0 -> 0; matrix products, arithmetic and copies ran while one was open for 32% -> 0% of each run, Pallas kernels for 0% -> 0%
where the time goes in v1:
time: 48.1 us; the launch traced here: 47.8 us
  Pallas kernels  38.5 us (80%)
  local copies, waits for them, and re-layouts  7.41 us (15%)
  other arithmetic  1.25 us (3%)
  between operations  0.64 us (1%)
    pallas_call x1, Pallas kernels, shards(): pl.pallas_call(functools.partial(kernel, n, scale), out_shape=out_shape,...  38.5 us
    unnamed x5, local copies, waits for them, and re-layouts  7.41 us
    mul x1, other arithmetic, shards(): half = ((levels.astype(F32) - 1.0) * 0.5).reshape(1, ch)  1.25 us

profile of v1, /device:TPU:0, one launch (start us, length us, event | category | flops | bytes accessed | tf_op | source)
XLA Modules:
  0.0 47.8 jit_solution(555304326141368700)
XLA Ops:
  0.6 1.2 %add_multiply_fusion = f32[256]{0:T(256)} fusion(s32[256]{0:T(256)} %param.16), kind=kLoop, calls=%fused_computation | loop fusion | flops 768 | bytes 2048 | tf_op jit(solution)/shard_map/mul | solution.py:430
  1.9 38.5 %shard_map.128 = (bf16[2,12,8,256]{3,2,1,0:T(8,128)(2,1)}, bf16[1,6,4,256]{3,2,1,0:T(4,128)(2,1)}, f32[128,256]{1,0:T(8,128)}, f32[48,256]{1,0:T(8,128)}, f32[16,2048]{1,0:T(8,128)}) custom-call(bf16[2,12,8,256]{3,2,1,0:T(8,128)(2,1)} %vf.1, bf16[2,12,8,256]{3,2,1,0:T(8,128)(2,1)} %ct.1, bf16[6912,256]{1,0:T(8,128)(2,1)} %we.1, bf16[2048,256]{1,0:T(8,128)(2,1)} %wd.1, ...), custom_call_target="tpu_custom_call" | custom-call | tf_op jit(solution)/shard_map/pallas_call | solution.py:460
  40.4 1.5 %copy.19 = bf16[2,12,8,256]{3,2,1,0:T(8,128)(2,1)} copy(bf16[2,12,8,256]{3,2,1,0:T(8,128)(2,1)} %get-tuple-element.10) | data formatting | bytes 196608
  41.9 1.3 %copy.20 = bf16[1,6,4,256]{3,2,1,0:T(4,128)(2,1)} copy(bf16[1,6,4,256]{3,2,1,0:T(4,128)(2,1)} %get-tuple-element.11) | data formatting | bytes 24576
  43.3 1.6 %copy.21 = f32[128,256]{1,0:T(8,128)} copy(f32[128,256]{1,0:T(8,128)} %get-tuple-element.12) | data formatting | bytes 262144
  44.8 1.4 %copy.22 = f32[48,256]{1,0:T(8,128)} copy(f32[48,256]{1,0:T(8,128)} %get-tuple-element.13) | data formatting | bytes 98304
  46.2 1.6 %copy.23 = f32[16,2048]{1,0:T(8,128)} copy(f32[16,2048]{1,0:T(8,128)} %get-tuple-element.14) | data formatting | bytes 262144

commit v2 on v1

v2 whole, which is shorter than its diff:
```python
import functools
import math

import jax
import jax.numpy as jnp
import numpy as np
from jax import lax
from jax.experimental import pallas as pl
from jax.experimental.pallas import tpu as pltpu
from jax.sharding import PartitionSpec as P

two_pi = 2.0 * math.pi
BF = jnp.bfloat16
F32 = jnp.float32
MESH = pl.DeviceIdType.MESH

HALO_V, HALO_C, HALO_N = 0, 1, 2
LAT, CGR, STK, DEP, UPS = 0, 1, 2, 3, 4

NEAR = (1, 2, -1, -2, -3)


def mm(a, b):
    return jnp.dot(a, b, preferred_element_type=F32)


def mm_nt(a, b):
    return lax.dot_general(a, b, (((1,), (1,)), ((), ())), preferred_element_type=F32)


def mm_tn(a, b):
    return lax.dot_general(a, b, (((0,), (0,)), ((), ())), preferred_element_type=F32)


def depth_permutation(rows, cols):
    order = np.arange(2 * rows * cols).reshape(2, rows // 2, 2, cols // 2, 2)
    order = order.transpose(0, 2, 4, 1, 3).reshape(-1)
    picks = np.zeros((order.size, order.size), np.float32)
    picks[np.arange(order.size), order] = 1.0
    return picks


def kernel(
    n, scale, vf, ct, we, wd, wc, wu, wx, levels, perm,
    vg_out, code_out, down_out, coarse_out, up_out,
    vbuf, cbuf, ebuf, we_v, wx_v, wd_v, wc_v, wu_v, perm_v, level_v,
    lat, cgr, cod, fac, pre, lgr, stk_mine, stk_all, dep_mine, dep_all, up_mine, up_all, coarse_v, whole_v,
    hal_s, hal_r, msg_s, msg_r, fwd_s, load_sem,
):
    frames, rows, width, ch = vf.shape
    fine = frames * rows * width
    cells = fine // 8
    nb, _, wb = stk_mine.shape
    rep = n // nb
    me = lax.axis_index("tm")

    def peer_of(k):
        return lax.rem(me + k, n)

    barrier = pltpu.get_barrier_semaphore()

    @pl.loop(1, n)
    def _(k):
        pl.semaphore_signal(barrier, inc=1, device_id={"tm": peer_of(k)}, device_id_type=MESH)

    inner = pl.ds(1, rows)
    third = we.shape[0] // 3
    loads = [
        pltpu.make_async_copy(vf, vbuf.at[2:4, inner], load_sem.at[0]),
        pltpu.make_async_copy(ct, cbuf.at[0:2, inner], load_sem.at[1]),
    ]
    for k, part in enumerate((2, 1, 0)):
        span = pl.ds(part * third, third)
        loads.append(pltpu.make_async_copy(we.at[span], we_v.at[span], load_sem.at[2 + 2 * k]))
        loads.append(pltpu.make_async_copy(wx.at[span], wx_v.at[span], load_sem.at[3 + 2 * k]))
    small = [
        pltpu.make_async_copy(src, dst, load_sem.at[8 + k])
        for k, (src, dst) in enumerate(
            ((perm, perm_v), (wd, wd_v), (wu, wu_v), (wc, wc_v), (levels, level_v))
        )
    ]
    for load in loads + small:
        load.start()

    def halo(kind, src, dst, peer):
        return pltpu.make_async_remote_copy(
            src_ref=src, dst_ref=dst, send_sem=hal_s.at[kind], recv_sem=hal_r.at[kind],
            device_id={"tm": peer}, device_id_type=MESH,
        )

    def message(kind, src, dst, peer, source, sends=None):
        return pltpu.make_async_remote_copy(
            src_ref=src, dst_ref=dst,
            send_sem=msg_s.at[kind, peer] if sends is None else sends,
            recv_sem=msg_r.at[kind, source],
            device_id={"tm": peer}, device_id_type=MESH,
        )

    def send_v():
        return halo(HALO_V, vf, vbuf.at[0:2, inner], me + 1)

    def send_c():
        return halo(HALO_C, ct, cbuf.at[2:4, inner], me - 1)

    def send_n():
        return halo(HALO_N, vf, vbuf.at[4:6, inner], me - 1)

    for buf in (vbuf, cbuf, ebuf):
        edge = jnp.zeros((buf.shape[0], 1, width, ch), BF)
        buf[:, 0:1] = edge
        buf[:, rows + 1 : rows + 2] = edge
    blank = jnp.zeros((2, rows, width, ch), BF)

    @pl.when(me == 0)
    def _():
        vbuf[0:2, 1 : rows + 1] = blank

    @pl.when(me == n - 1)
    def _():
        cbuf[2:4, 1 : rows + 1] = blank
        vbuf[4:6, 1 : rows + 1] = blank

    lat[0:2] = jnp.zeros((2, cells, ch), BF)
    lat[n + 2 : n + 5] = jnp.zeros((3, cells, ch), BF)
    cgr[n : n + 3] = jnp.zeros((3, cells, ch), BF)
    pre[n : n + 2] = jnp.zeros((2, cells, ch), BF)

    pl.semaphore_wait(barrier, n - 1)

    @pl.when(me < n - 1)
    def _():
        send_v().start()

    @pl.when(me > 0)
    def _():
        send_c().start()
        send_n().start()

    def taps(buf, at):
        return jnp.concatenate(
            [buf[at : at + 2, q : q + rows].reshape(fine, ch) for q in range(3)], axis=1
        )

    def past(buf, at, weight, p):
        left = taps(buf, at + p)
        out = []
        for r in range(3):
            right = jnp.concatenate(
                [weight[pl.ds(((3 * p + q) * 3 + r) * ch, ch)] for q in range(3)], axis=0
            )
            out.append(mm(left, right))
        return out

    def future(buf, at, weight, p):
        left = taps(buf, at + p)
        out = []
        for r in range(3):
            right = jnp.concatenate(
                [
                    weight[pl.ds((((2 - p) * 3 + 2 - q) * 3 + 2 - r) * ch, ch)]
                    for q in range(3)
                ],
                axis=1,
            )
            out.append(mm_nt(left, right))
        return out

    def added(a, b):
        return [x + y for x, y in zip(a, b)]

    lane = lax.broadcasted_iota(jnp.int32, (fine // width, width, ch), 1)

    def aligned(parts):
        a, b, c = [x.reshape(fine // width, width, ch) for x in parts]
        a = jnp.where(lane == 0, 0.0, pltpu.roll(a, 1, 1))
        c = jnp.where(lane == width - 1, 0.0, pltpu.roll(c, width - 1, 1))
        return (a + b + c).reshape(fine, ch)

    loads[0].wait()
    loads[2].wait()
    enc = past(vbuf, 0, we_v, 2)
    loads[1].wait()
    loads[7].wait()
    loads[3].wait()
    dec = future(cbuf, 0, wx_v, 0)
    loads[4].wait()
    loads[6].wait()

    @pl.when(me > 0)
    def _():
        send_v().wait_recv()

    enc = added(enc, past(vbuf, 0, we_v, 1))
    enc = added(enc, past(vbuf, 0, we_v, 0))
    pre_enc = aligned(enc)
    sig = jax.nn.sigmoid(pre_enc)
    own = vbuf[2:4, 1 : rows + 1].reshape(fine, ch).astype(F32)
    hidden = (own + pre_enc * sig).astype(BF)

    def slope_of(x, s):
        return s * (1.0 + x * (1.0 - s))

    slope = slope_of(pre_enc, sig)

    for load in small:
        load.wait()

    def regroup(field, store):
        moved = mm(perm_v[0], field)
        blocks = [moved[b * cells : (b + 1) * cells].astype(BF) for b in range(8)]
        per = nb // 8
        for b in range(8):
            for h in range(per):
                store[b * per + h] = blocks[b][:, h * wb : (h + 1) * wb]
        return jnp.concatenate(blocks, axis=1)

    buddy = me + 1 - 2 * lax.rem(me, 2)

    def slot_send(buf, kind, slot, peer):
        return message(kind, buf.at[slot], buf.at[slot], peer, me)

    def inside(k):
        return (me + k >= 0) & (me + k < n)

    def spread(buf, kind, slot, act):
        for k in NEAR:
            @pl.when(inside(k))
            def _():
                act(slot_send(buf, kind, slot, me + k))

        @pl.loop(1, n // 2)
        def _(k):
            peer = lax.rem(me + 2 * k, n)
            @pl.when(((peer - me) != 2) & ((peer - me) != -2))
            def _():
                act(slot_send(buf, kind, slot, peer))

    def near_odd(diff):
        return (diff == 1) | (diff == -1) | (diff == -3)

    def arrival(buf, kind, shift, source):
        return message(kind, buf.at[me + shift], buf.at[source + shift], me, source)

    def forward(buf, kind, shift, source):
        slot = source + shift
        return message(kind, buf.at[slot], buf.at[slot], buddy, source, fwd_s.at[kind, source])

    def relay(buf, kind, shift, near):
        @pl.loop(1, n // 2)
        def _(k):
            source = lax.rem(me + n - 2 * k, n)
            diff = source - me
            done = functools.reduce(jnp.logical_or, [diff == d for d in near])

            @pl.when(jnp.logical_not(done))
            def _():
                arrival(buf, kind, shift, source).wait_recv()

            @pl.when(jnp.logical_not(near_odd(buddy - source)))
            def _():
                forward(buf, kind, shift, source).start()

    def collect(buf, kind, shift, near):
        @pl.loop(0, n // 2)
        def _(k):
            source = lax.rem(buddy + 2 * k, n)
            diff = source - me
            done = functools.reduce(jnp.logical_or, [diff == d for d in near])

            @pl.when(jnp.logical_not(done))
            def _():
                arrival(buf, kind, shift, source).wait_recv()

    def start(copy):
        copy.start()

    def wait_send(copy):
        copy.wait_send()

    lat[me + 2] = mm(regroup(hidden, stk_mine), wd_v[...]).astype(BF)
    spread(lat, LAT, me + 2, start)

    loads[5].wait()

    @pl.when(me < n - 1)
    def _():
        send_c().wait_recv()

    dec = added(dec, future(cbuf, 0, wx_v, 1))
    dec = added(dec, future(cbuf, 0, wx_v, 2))
    own_c = cbuf[0:2, 1 : rows + 1].reshape(fine, ch).astype(F32)
    depth = regroup((own_c + aligned(dec)).astype(BF), dep_mine)
    cgr[me] = mm_nt(depth, wu_v[...]).astype(BF)
    spread(cgr, CGR, me, start)

    def block_send(kind, mine, everyone, peer):
        return message(kind, mine.at[peer // rep], everyone.at[me], peer, me)

    @pl.loop(1, n)
    def _(k):
        block_send(DEP, dep_mine, dep_all, peer_of(k)).start()

    @pl.loop(1, n)
    def _(k):
        block_send(STK, stk_mine, stk_all, peer_of(k)).start()

    dep_all[me] = dep_mine[me // rep]
    stk_all[me] = stk_mine[me // rep]

    @pl.when(me < n - 1)
    def _():
        send_n().wait_recv()

    ahead = past(vbuf, 2, we_v, 0)
    ahead = added(ahead, past(vbuf, 2, we_v, 1))
    ahead = aligned(added(ahead, past(vbuf, 2, we_v, 2)))
    slope_next = slope_of(ahead, jax.nn.sigmoid(ahead))

    half = ((level_v[...].astype(F32) - 1.0) * 0.5).reshape(1, ch)

    def coder(frame, count):
        columns = jnp.concatenate(
            [lat[pl.ds(frame + p, count)].reshape(count * cells, ch) for p in range(3)], axis=1
        )
        squashed = jnp.tanh(mm(columns, wc_v[...]))
        bounded = half * squashed
        codes = ((bounded - jnp.sin(two_pi * bounded) / two_pi) / half).astype(BF)
        return codes, (1.0 - jnp.cos(two_pi * bounded)) * (1.0 - squashed * squashed)

    wc_flip = jnp.concatenate([wc_v[pl.ds((2 - p) * ch, ch)] for p in range(3)], axis=1)

    lat_near = (-1, -2, 1, 2, 3)
    cgr_near = (1, 2, 3)
    for k in lat_near:
        @pl.when(inside(k))
        def _():
            arrival(lat, LAT, 2, me + k).wait_recv()

    codes, factor = coder(me, 4)
    code_out[...] = codes[0:cells].reshape(code_out.shape)
    for k in cgr_near:
        @pl.when(inside(k))
        def _():
            arrival(cgr, CGR, 0, me + k).wait_recv()

    ahead_grad = cgr[pl.ds(me, 4)].reshape(4 * cells, ch).astype(F32) * factor
    later = jnp.concatenate(
        [ahead_grad[p * cells : (p + 2) * cells].astype(BF) for p in range(3)], axis=1
    )
    grad_lat = mm_nt(later, wc_flip).astype(BF)

    deep_grad = mm_nt(grad_lat, wd_v[...])
    back = perm_v[1]
    hidden_grads = []
    for frame in range(2):
        deep_rows = jnp.concatenate(
            [
                deep_grad[frame * cells : (frame + 1) * cells, b * ch : (b + 1) * ch]
                for b in range(8)
            ],
            axis=0,
        )
        high = deep_rows.astype(BF)
        rest = deep_rows - high.astype(F32)
        middle = rest.astype(BF)
        low = (rest - middle.astype(F32)).astype(BF)
        hidden_grads.append(mm(back, high) + (mm(back, middle) + mm(back, low)))
    for frame, weight in enumerate((slope, slope_next)):
        ebuf[2 * frame : 2 * frame + 2, 1 : rows + 1] = (
            (hidden_grads[frame] * weight).astype(BF).reshape(2, rows, width, ch)
        )

    relay(lat, LAT, 2, lat_near)
    bck = future(ebuf, 0, we_v, 0)
    bck = added(bck, future(ebuf, 0, we_v, 1))
    bck = added(bck, future(ebuf, 0, we_v, 2))
    vg_out[...] = (hidden_grads[0] + aligned(bck)).astype(BF).reshape(vg_out.shape)
    relay(cgr, CGR, 0, cgr_near)

    collect(lat, LAT, 2, lat_near)
    step = 4
    total = n * cells

    @pl.loop(0, n // step)
    def _(k):
        at = k * step
        codes, factor = coder(at, step)
        cod[pl.ds(at, step)] = codes.reshape(step, cells, ch)
        fac[pl.ds(at, step)] = factor.reshape(step, cells, ch)

    @pl.loop(1, n)
    def _(k):
        source = peer_of(k)
        message(DEP, dep_mine.at[0], dep_all.at[source], me, source).wait_recv()

    up_part = mm_tn(cod[...].reshape(total, ch), dep_all[...].reshape(total, wb)) * scale
    block_rows = up_mine.shape[1]
    up_mine[...] = up_part.reshape(up_mine.shape)
    up_rows = ch // n
    mine = lax.rem(me, rep)
    my_block = me // rep

    def up_target(k):
        return mine + rep * lax.rem(my_block + k, nb)

    def up_send(peer):
        return message(
            UPS, up_mine.at[peer * up_rows // block_rows], up_all.at[my_block], peer, me
        )

    @pl.loop(1, nb)
    def _(k):
        up_send(up_target(k)).start()

    up_all[my_block] = up_mine[me * up_rows // block_rows]

    def take_rows(buf, at, out):
        count = out.shape[0]
        if count % 8 == 0:
            out[...] = buf[pl.ds(pl.multiple_of(at, 8), count)]
        else:
            for k in range(count):
                out[pl.ds(k, 1)] = buf[pl.ds(at + k, 1)]

    collect(cgr, CGR, 0, cgr_near)
    pre[0:n] = (cgr[0:n].astype(F32) * fac[...]).astype(BF)
    pre_all = pre[0:n].reshape(total, ch)
    for p in range(3):
        coarse_v[pl.ds(p * ch, ch)] = mm_tn(lat[p : p + n].reshape(total, ch), pre_all) * scale
    take_rows(coarse_v, me * coarse_out.shape[0], coarse_out)
    later_all = jnp.concatenate([pre[p : p + n].reshape(total, ch) for p in range(3)], axis=1)
    lgr[...] = mm_nt(later_all, wc_flip).astype(BF).reshape(lgr.shape)

    @pl.loop(1, n)
    def _(k):
        source = peer_of(k)
        message(STK, stk_mine.at[0], stk_all.at[source], me, source).wait_recv()

    whole_v[0:wb, 0:ch] = (
        mm_tn(stk_all[...].reshape(total, wb), lgr[...].reshape(total, ch)) * scale
    )
    take_rows(whole_v.at[:, pl.ds(0, ch)], mine * down_out.shape[0], down_out)

    @pl.loop(1, nb)
    def _(k):
        source = up_target(k)
        message(UPS, up_mine.at[0], up_all.at[source // rep], me, source).wait_recv()

    up_at = lax.rem(me * up_rows, block_rows)
    for b in range(nb):
        take_rows(up_all.at[b], up_at, up_out.at[:, pl.ds(b * wb, wb)])

    @pl.when(me < n - 1)
    def _():
        send_v().wait_send()

    @pl.when(me > 0)
    def _():
        send_c().wait_send()
        send_n().wait_send()

    for buf, kind, shift in ((lat, LAT, 2), (cgr, CGR, 0)):
        spread(buf, kind, me + shift, wait_send)

        @pl.loop(1, n // 2)
        def _(k):
            source = lax.rem(me + n - 2 * k, n)

            @pl.when(jnp.logical_not(near_odd(buddy - source)))
            def _():
                forward(buf, kind, shift, source).wait_send()

    @pl.loop(1, n)
    def _(k):
        block_send(DEP, dep_mine, dep_all, peer_of(k)).wait_send()
        block_send(STK, stk_mine, stk_all, peer_of(k)).wait_send()

    @pl.loop(1, nb)
    def _(k):
        up_send(up_target(k)).wait_send()


def tail(*refs):
    sems = refs[-1]
    count = len(refs) // 2
    copies = [pltpu.make_async_copy(refs[k], refs[count + k], sems.at[k]) for k in range(count)]
    for copy in copies:
        copy.start()
    for copy in copies:
        copy.wait()


def shards(n, vf, ct, we, wd, wc, wu, wx, levels):
    frames, rows, width, ch = vf.shape
    deep = wd.shape[0]
    fine = frames * rows * width
    cells = fine // 8
    wb = max(128, deep // n)
    nb = deep // wb
    up_rows = ch // n
    block_rows = max(8, up_rows)
    scale = 1.0 / math.sqrt(n * fine)
    picks = depth_permutation(rows, width)
    perm = jnp.asarray(np.stack([picks, picks.T]), BF)
    anywhere = pl.BlockSpec(memory_space=pl.ANY)
    results = (
        (vf.shape, BF),
        ((frames // 2, rows // 2, width // 2, ch), BF),
        ((deep // n, ch), F32),
        ((wc.shape[0] // n, ch), F32),
        ((up_rows, deep), F32),
    )
    four = (4, rows + 2, width, ch)
    scratch = [
        pltpu.VMEM((6, rows + 2, width, ch), BF), pltpu.VMEM(four, BF), pltpu.VMEM(four, BF),
        pltpu.VMEM(we.shape, BF), pltpu.VMEM(wx.shape, BF), pltpu.VMEM(wd.shape, BF),
        pltpu.VMEM(wc.shape, BF), pltpu.VMEM(wu.shape, BF), pltpu.VMEM(perm.shape, BF),
        pltpu.VMEM(levels.shape, jnp.int32),
        pltpu.VMEM((n + 5, cells, ch), BF), pltpu.VMEM((n + 3, cells, ch), BF),
        pltpu.VMEM((n, cells, ch), BF), pltpu.VMEM((n, cells, ch), F32),
        pltpu.VMEM((n + 2, cells, ch), BF), pltpu.VMEM((n, cells, ch), BF),
        pltpu.VMEM((nb, cells, wb), BF), pltpu.VMEM((n, cells, wb), BF),
        pltpu.VMEM((nb, cells, wb), BF), pltpu.VMEM((n, cells, wb), BF),
        pltpu.VMEM((ch // block_rows, block_rows, wb), F32),
        pltpu.VMEM((nb, block_rows, wb), F32),
        pltpu.VMEM(wc.shape, F32), pltpu.VMEM((wb, ch), F32),
        pltpu.SemaphoreType.DMA((3,)), pltpu.SemaphoreType.DMA((3,)),
        pltpu.SemaphoreType.DMA((5, n)), pltpu.SemaphoreType.DMA((5, n)),
        pltpu.SemaphoreType.DMA((2, n)), pltpu.SemaphoreType.DMA((13,)),
    ]
    held = pl.pallas_call(
        functools.partial(kernel, n, scale),
        out_shape=tuple(pltpu.VMEM(*result) for result in results),
        in_specs=[anywhere] * 9,
        out_specs=(pl.BlockSpec(memory_space=pltpu.VMEM),) * 5,
        scratch_shapes=scratch,
        compiler_params=pltpu.CompilerParams(collective_id=0, has_side_effects=True),
    )(vf, ct, we, wd, wc, wu, wx, levels, perm)
    return pl.pallas_call(
        tail,
        out_shape=tuple(jax.ShapeDtypeStruct(*result) for result in results),
        in_specs=[anywhere] * 5,
        out_specs=(anywhere,) * 5,
        scratch_shapes=[pltpu.SemaphoreType.DMA((5,))],
    )(*[pltpu.with_memory_space_constraint(part, pltpu.VMEM) for part in held])


def solution(mesh):
    placed = (P("tm", "grp", None, None), P("tm", "grp", None, None), P(), P(), P(), P(), P(), P())
    return jax.shard_map(
        functools.partial(shards, mesh.shape["tm"]),
        mesh=mesh,
        in_specs=placed,
        out_specs=(
            P("tm", "grp", None, None),
            P("tm", "grp", None, None),
            P(("grp", "tm"), None),
            P(("grp", "tm"), None),
            P(("grp", "tm"), None),
        ),
        check_vma=False,
    )
```

time: 48.1 us -> 31.6 us (0.66)
  Pallas kernels: 38.5 us -> 30.8 us
  local copies, waits for them, and re-layouts: 7.41 us -> 0 us
  other arithmetic: 1.25 us -> 0 us
    pallas_call x1 -> x2, Pallas kernels: 38.5 us -> 30.8 us  [the longest x1 30 us: shards(): pl.pallas_call(functools.partial(kernel, n, scale), out_shape=tuple((pltp...]
    unnamed x5 -> x0, local copies, waits for them, and re-layouts: 7.41 us -> none
    mul x1 -> x0, other arithmetic: 1.25 us -> none  [shards(): half = ((levels.astype(F32) - 1.0) * 0.5).reshape(1, ch)]
where the time goes in v2:
time: 31.6 us; the launch traced here: 31.4 us
  Pallas kernels  30.8 us (97%)
  between operations  0.64 us (2%)
    pallas_call x1, Pallas kernels, shards(): pl.pallas_call(functools.partial(kernel, n, scale), out_shape=tuple((pltp...  30 us
    pallas_call x1, Pallas kernels, shards(): pl.pallas_call(tail, out_shape=tuple((jax.ShapeDtypeStruct(*result) for r...  0.8 us

profile of v2, /device:TPU:0, one launch (start us, length us, event | category | flops | bytes accessed | tf_op | source)
XLA Modules:
  0.0 31.4 jit_solution(14783752424125058226)
XLA Ops:
  0.6 30.0 %shard_map.128 = (bf16[2,12,8,256]{3,2,1,0:T(8,128)(2,1)S(1)}, bf16[1,6,4,256]{3,2,1,0:T(4,128)(2,1)S(1)}, f32[128,256]{1,0:T(8,128)S(1)}, f32[48,256]{1,0:T(8,128)S(1)}, f32[16,2048]{1,0:T(8,128)S(1)}) custom-call(bf16[2,12,8,256]{3,2,1,0:T(8,128)(2,1)} %vf.1, bf16[2,12,8,256]{3,2,1,0:T(8,128)(2,1)} %ct.1, bf16[6912,256]{1,0:T(8,128)(2,1)} %we.1, ...), custom_call_target="tpu_custom_call" | custom-call | tf_op jit(solution)/shard_map/pallas_call | solution.py:531
  30.6 0.8 %shard_map.129 = (bf16[2,12,8,256]{3,2,1,0:T(8,128)(2,1)}, bf16[1,6,4,256]{3,2,1,0:T(4,128)(2,1)}, f32[128,256]{1,0:T(8,128)}, f32[48,256]{1,0:T(8,128)}, f32[16,2048]{1,0:T(8,128)}) custom-call(bf16[2,12,8,256]{3,2,1,0:T(8,128)(2,1)S(1)} %get-tuple-element.10.refs_0_, bf16[1,6,4,256]{3,2,1,0:T(4,128)(2,1)S(1)} %get-tuple-element.11.refs_1_, ...), custom_call_target="tpu_custom_call" | custom-call | tf_op jit(solution)/shard_map/pallas_call | solution.py:539

commit v3 on v2

--- a/solution.py
+++ b/solution.py
@@ -15,7 +15,11 @@
 MESH = pl.DeviceIdType.MESH
 
 HALO_V, HALO_C, HALO_N = 0, 1, 2
-LAT, CGR, STK, DEP, UPS = 0, 1, 2, 3, 4
+LAT, CGR = 0, 1
+STK, DEP, UPS = 0, 1, 2
+
+SINE = [(-1.0) ** k / math.factorial(2 * k + 1) for k in range(7)]
+COSINE = [(-1.0) ** k / math.factorial(2 * k) for k in range(7)]
 
 NEAR = (1, 2, -1, -2, -3)
 
@@ -30,6 +34,16 @@
 
 def mm_tn(a, b):
     return lax.dot_general(a, b, (((0,), (0,)), ((), ())), preferred_element_type=F32)
+
+
+def half_turn(x):
+    angle = (x - jnp.round(x)) * math.pi
+    square = angle * angle
+    sine, cosine = SINE[-1], COSINE[-1]
+    for a, b in zip(SINE[-2::-1], COSINE[-2::-1]):
+        sine = sine * square + a
+        cosine = cosine * square + b
+    return sine * angle, cosine
 
 
 def depth_permutation(rows, cols):
@@ -45,7 +59,7 @@
     vg_out, code_out, down_out, coarse_out, up_out,
     vbuf, cbuf, ebuf, we_v, wx_v, wd_v, wc_v, wu_v, perm_v, level_v,
     lat, cgr, cod, fac, pre, lgr, stk_mine, stk_all, dep_mine, dep_all, up_mine, up_all, coarse_v, whole_v,
-    hal_s, hal_r, msg_s, msg_r, fwd_s, load_sem,
+    acc_e, acc_d, hal_s, hal_r, msg_s, msg_r, fwd_s, all_s, all_r, load_sem, met,
 ):
     frames, rows, width, ch = vf.shape
     fine = frames * rows * width
@@ -57,11 +71,32 @@
     def peer_of(k):
         return lax.rem(me + k, n)
 
+    odd = lax.rem(me, 2)
+    buddy = me + 1 - 2 * odd
+    other = me - 1 + 2 * odd
+    has_other = (other >= 0) & (other < n)
+    dims = n.bit_length() - 1
+
+    def partner(d):
+        return me + (1 - 2 * lax.rem(me // 2**d, 2)) * 2**d
+
     barrier = pltpu.get_barrier_semaphore()
-
-    @pl.loop(1, n)
-    def _(k):
-        pl.semaphore_signal(barrier, inc=1, device_id={"tm": peer_of(k)}, device_id_type=MESH)
+    for d in range(dims):
+        pl.semaphore_signal(barrier, inc=1, device_id={"tm": partner(d)}, device_id_type=MESH)
+
+    @pl.when(has_other)
+    def _():
+        pl.semaphore_signal(barrier, inc=1, device_id={"tm": other}, device_id_type=MESH)
+
+    def tell(d):
+        if d < dims:
+            pl.semaphore_signal(
+                met.at[d], inc=1, device_id={"tm": partner(d)}, device_id_type=MESH
+            )
+
+    def hear(d):
+        if d < dims:
+            pl.semaphore_wait(met.at[d], 1)
 
     inner = pl.ds(1, rows)
     third = we.shape[0] // 3
@@ -96,6 +131,15 @@
             device_id={"tm": peer}, device_id_type=MESH,
         )
 
+    def block(kind, src, dst, peer):
+        return pltpu.make_async_remote_copy(
+            src_ref=src, dst_ref=dst, send_sem=all_s.at[kind], recv_sem=all_r.at[kind],
+            device_id={"tm": peer}, device_id_type=MESH,
+        )
+
+    def all_blocks(kind, buf, count):
+        return block(kind, buf.at[pl.ds(0, count)], buf.at[pl.ds(0, count)], buddy)
+
     def send_v():
         return halo(HALO_V, vf, vbuf.at[0:2, inner], me + 1)
 
@@ -123,9 +167,11 @@
     lat[0:2] = jnp.zeros((2, cells, ch), BF)
     lat[n + 2 : n + 5] = jnp.zeros((3, cells, ch), BF)
     cgr[n : n + 3] = jnp.zeros((3, cells, ch), BF)
-    pre[n : n + 2] = jnp.zeros((2, cells, ch), BF)
-
-    pl.semaphore_wait(barrier, n - 1)
+    pre[0:2] = jnp.zeros((2, cells, ch), BF)
+    pre[n + 2 : n + 4] = jnp.zeros((2, cells, ch), BF)
+
+    pl.semaphore_wait(barrier, jnp.where(has_other, dims + 1, dims))
+    tell(0)
 
     @pl.when(me < n - 1)
     def _():
@@ -141,23 +187,29 @@
             [buf[at : at + 2, q : q + rows].reshape(fine, ch) for q in range(3)], axis=1
         )
 
-    def past(buf, at, weight, p):
-        left = taps(buf, at + p)
+    def past(buf, at, weight, parts):
+        left = jnp.concatenate([taps(buf, at + p) for p in parts], axis=1)
         out = []
         for r in range(3):
             right = jnp.concatenate(
-                [weight[pl.ds(((3 * p + q) * 3 + r) * ch, ch)] for q in range(3)], axis=0
+                [
+                    weight[pl.ds(((3 * p + q) * 3 + r) * ch, ch)]
+                    for p in parts
+                    for q in range(3)
+                ],
+                axis=0,
             )
             out.append(mm(left, right))
         return out
 
-    def future(buf, at, weight, p):
-        left = taps(buf, at + p)
+    def future(buf, at, weight, parts):
+        left = jnp.concatenate([taps(buf, at + p) for p in parts], axis=1)
         out = []
         for r in range(3):
             right = jnp.concatenate(
                 [
                     weight[pl.ds((((2 - p) * 3 + 2 - q) * 3 + 2 - r) * ch, ch)]
+                    for p in parts
                     for q in range(3)
                 ],
                 axis=1,
@@ -165,8 +217,12 @@
             out.append(mm_nt(left, right))
         return out
 
-    def added(a, b):
-        return [x + y for x, y in zip(a, b)]
+    def keep(acc, parts):
+        for r in range(3):
+            acc[r] = parts[r]
+
+    def added(acc, parts):
+        return [acc[r] + parts[r] for r in range(3)]
 
     lane = lax.broadcasted_iota(jnp.int32, (fine // width, width, ch), 1)
 
@@ -178,11 +234,14 @@
 
     loads[0].wait()
     loads[2].wait()
-    enc = past(vbuf, 0, we_v, 2)
+    keep(acc_e, past(vbuf, 0, we_v, (2,)))
+    hear(0)
+    tell(1)
     loads[1].wait()
-    loads[7].wait()
     loads[3].wait()
-    dec = future(cbuf, 0, wx_v, 0)
+    keep(acc_d, future(cbuf, 0, wx_v, (0,)))
+    hear(1)
+    tell(2)
     loads[4].wait()
     loads[6].wait()
 
@@ -190,8 +249,9 @@
     def _():
         send_v().wait_recv()
 
-    enc = added(enc, past(vbuf, 0, we_v, 1))
-    enc = added(enc, past(vbuf, 0, we_v, 0))
+    hear(2)
+    tell(3)
+    enc = added(acc_e, past(vbuf, 0, we_v, (1, 0)))
     pre_enc = aligned(enc)
     sig = jax.nn.sigmoid(pre_enc)
     own = vbuf[2:4, 1 : rows + 1].reshape(fine, ch).astype(F32)
@@ -199,8 +259,6 @@
 
     def slope_of(x, s):
         return s * (1.0 + x * (1.0 - s))
-
-    slope = slope_of(pre_enc, sig)
 
     for load in small:
         load.wait()
@@ -214,7 +272,6 @@
                 store[b * per + h] = blocks[b][:, h * wb : (h + 1) * wb]
         return jnp.concatenate(blocks, axis=1)
 
-    buddy = me + 1 - 2 * lax.rem(me, 2)
 
     def slot_send(buf, kind, slot, peer):
         return message(kind, buf.at[slot], buf.at[slot], peer, me)
@@ -222,12 +279,13 @@
     def inside(k):
         return (me + k >= 0) & (me + k < n)
 
-    def spread(buf, kind, slot, act):
+    def spread_near(buf, kind, slot, act):
         for k in NEAR:
             @pl.when(inside(k))
             def _():
                 act(slot_send(buf, kind, slot, me + k))
 
+    def spread_rest(buf, kind, slot, act):
         @pl.loop(1, n // 2)
         def _(k):
             peer = lax.rem(me + 2 * k, n)
@@ -250,7 +308,7 @@
         def _(k):
             source = lax.rem(me + n - 2 * k, n)
             diff = source - me
-            done = functools.reduce(jnp.logical_or, [diff == d for d in near])
+            done = functools.reduce(jnp.logical_or, [diff == d for d in near], False)
 
             @pl.when(jnp.logical_not(done))
             def _():
@@ -265,7 +323,7 @@
         def _(k):
             source = lax.rem(buddy + 2 * k, n)
             diff = source - me
-            done = functools.reduce(jnp.logical_or, [diff == d for d in near])
+            done = functools.reduce(jnp.logical_or, [diff == d for d in near], False)
 
             @pl.when(jnp.logical_not(done))
             def _():
@@ -278,28 +336,35 @@
         copy.wait_send()
 
     lat[me + 2] = mm(regroup(hidden, stk_mine), wd_v[...]).astype(BF)
-    spread(lat, LAT, me + 2, start)
+    hear(3)
+    for d in range(4, dims):
+        tell(d)
+        hear(d)
+    spread_near(lat, LAT, me + 2, start)
+    spread_rest(lat, LAT, me + 2, start)
 
     loads[5].wait()
+    loads[7].wait()
 
     @pl.when(me < n - 1)
     def _():
         send_c().wait_recv()
 
-    dec = added(dec, future(cbuf, 0, wx_v, 1))
-    dec = added(dec, future(cbuf, 0, wx_v, 2))
+    dec = added(acc_d, future(cbuf, 0, wx_v, (1, 2)))
     own_c = cbuf[0:2, 1 : rows + 1].reshape(fine, ch).astype(F32)
     depth = regroup((own_c + aligned(dec)).astype(BF), dep_mine)
     cgr[me] = mm_nt(depth, wu_v[...]).astype(BF)
-    spread(cgr, CGR, me, start)
+    spread_near(cgr, CGR, me, start)
 
     def block_send(kind, mine, everyone, peer):
-        return message(kind, mine.at[peer // rep], everyone.at[me], peer, me)
+        return block(kind, mine.at[peer // rep], everyone.at[me], peer)
 
     @pl.loop(1, n)
     def _(k):
         block_send(DEP, dep_mine, dep_all, peer_of(k)).start()
 
+    spread_rest(cgr, CGR, me, start)
+
     @pl.loop(1, n)
     def _(k):
         block_send(STK, stk_mine, stk_all, peer_of(k)).start()
@@ -307,16 +372,8 @@
     dep_all[me] = dep_mine[me // rep]
     stk_all[me] = stk_mine[me // rep]
 
-    @pl.when(me < n - 1)
-    def _():
-        send_n().wait_recv()
-
-    ahead = past(vbuf, 2, we_v, 0)
-    ahead = added(ahead, past(vbuf, 2, we_v, 1))
-    ahead = aligned(added(ahead, past(vbuf, 2, we_v, 2)))
-    slope_next = slope_of(ahead, jax.nn.sigmoid(ahead))
-
     half = ((level_v[...].astype(F32) - 1.0) * 0.5).reshape(1, ch)
+    inverse = 1.0 / half
 
     def coder(frame, count):
         columns = jnp.concatenate(
@@ -324,10 +381,29 @@
         )
         squashed = jnp.tanh(mm(columns, wc_v[...]))
         bounded = half * squashed
-        codes = ((bounded - jnp.sin(two_pi * bounded) / two_pi) / half).astype(BF)
-        return codes, (1.0 - jnp.cos(two_pi * bounded)) * (1.0 - squashed * squashed)
+        sine, cosine = half_turn(bounded)
+        codes = ((bounded - sine * cosine * (2.0 / two_pi)) * inverse).astype(BF)
+        return codes, (2.0 * sine * sine) * (1.0 - squashed * squashed)
 
     wc_flip = jnp.concatenate([wc_v[pl.ds((2 - p) * ch, ch)] for p in range(3)], axis=1)
+
+    @pl.when(me < n - 1)
+    def _():
+        send_n().wait_recv()
+
+    ahead = aligned(past(vbuf, 2, we_v, (0, 1, 2)))
+
+    def moved_exactly(perm, x):
+        high = x.astype(BF)
+        rest = x - high.astype(F32)
+        middle = rest.astype(BF)
+        low = (rest - middle.astype(F32)).astype(BF)
+        return mm(perm, high) + (mm(perm, middle) + mm(perm, low))
+
+    slopes = [
+        moved_exactly(perm_v[0], slope_of(x, s))
+        for x, s in ((pre_enc, sig), (ahead, jax.nn.sigmoid(ahead)))
+    ]
 
     lat_near = (-1, -2, 1, 2, 3)
     cgr_near = (1, 2, 3)
@@ -338,6 +414,8 @@
 
     codes, factor = coder(me, 4)
     code_out[...] = codes[0:cells].reshape(code_out.shape)
+    relay(lat, LAT, 2, lat_near)
+
     for k in cgr_near:
         @pl.when(inside(k))
         def _():
@@ -350,35 +428,27 @@
     grad_lat = mm_nt(later, wc_flip).astype(BF)
 
     deep_grad = mm_nt(grad_lat, wd_v[...])
-    back = perm_v[1]
-    hidden_grads = []
-    for frame in range(2):
-        deep_rows = jnp.concatenate(
+    deep_rows = [
+        jnp.concatenate(
             [
                 deep_grad[frame * cells : (frame + 1) * cells, b * ch : (b + 1) * ch]
                 for b in range(8)
             ],
             axis=0,
         )
-        high = deep_rows.astype(BF)
-        rest = deep_rows - high.astype(F32)
-        middle = rest.astype(BF)
-        low = (rest - middle.astype(F32)).astype(BF)
-        hidden_grads.append(mm(back, high) + (mm(back, middle) + mm(back, low)))
-    for frame, weight in enumerate((slope, slope_next)):
+        for frame in range(2)
+    ]
+    back = perm_v[1]
+    for frame in range(2):
         ebuf[2 * frame : 2 * frame + 2, 1 : rows + 1] = (
-            (hidden_grads[frame] * weight).astype(BF).reshape(2, rows, width, ch)
-        )
-
-    relay(lat, LAT, 2, lat_near)
-    bck = future(ebuf, 0, we_v, 0)
-    bck = added(bck, future(ebuf, 0, we_v, 1))
-    bck = added(bck, future(ebuf, 0, we_v, 2))
-    vg_out[...] = (hidden_grads[0] + aligned(bck)).astype(BF).reshape(vg_out.shape)
-    relay(cgr, CGR, 0, cgr_near)
+            mm(back, (deep_rows[frame] * slopes[frame]).astype(BF))
+            .astype(BF)
+            .reshape(2, rows, width, ch)
+        )
+    hidden_grad = moved_exactly(back, deep_rows[0])
 
     collect(lat, LAT, 2, lat_near)
-    step = 4
+    step = min(n, 16)
     total = n * cells
 
     @pl.loop(0, n // step)
@@ -388,10 +458,7 @@
         cod[pl.ds(at, step)] = codes.reshape(step, cells, ch)
         fac[pl.ds(at, step)] = factor.reshape(step, cells, ch)
 
-    @pl.loop(1, n)
-    def _(k):
-        source = peer_of(k)
-        message(DEP, dep_mine.at[0], dep_all.at[source], me, source).wait_recv()
+    all_blocks(DEP, dep_all, n - 1).wait_recv()
 
     up_part = mm_tn(cod[...].reshape(total, ch), dep_all[...].reshape(total, wb)) * scale
     block_rows = up_mine.shape[1]
@@ -404,9 +471,7 @@
         return mine + rep * lax.rem(my_block + k, nb)
 
     def up_send(peer):
-        return message(
-            UPS, up_mine.at[peer * up_rows // block_rows], up_all.at[my_block], peer, me
-        )
+        return block(UPS, up_mine.at[peer * up_rows // block_rows], up_all.at[my_block], peer)
 
     @pl.loop(1, nb)
     def _(k):
@@ -422,62 +487,59 @@
             for k in range(count):
                 out[pl.ds(k, 1)] = buf[pl.ds(at + k, 1)]
 
+    relay(cgr, CGR, 0, cgr_near)
+    bck = future(ebuf, 0, we_v, (0, 1, 2))
+    vg_out[...] = (hidden_grad + aligned(bck)).astype(BF).reshape(vg_out.shape)
     collect(cgr, CGR, 0, cgr_near)
-    pre[0:n] = (cgr[0:n].astype(F32) * fac[...]).astype(BF)
-    pre_all = pre[0:n].reshape(total, ch)
+    pre[2 : n + 2] = (cgr[0:n].astype(F32) * fac[...]).astype(BF)
+    long = (n + 2) * cells
+    shifted = jnp.concatenate(
+        [pre[2 - p : 2 - p + n + 2].reshape(long, ch) for p in range(3)], axis=1
+    )
+    coarse_all = mm_tn(lat[0 : n + 2].reshape(long, ch), shifted) * scale
     for p in range(3):
-        coarse_v[pl.ds(p * ch, ch)] = mm_tn(lat[p : p + n].reshape(total, ch), pre_all) * scale
+        coarse_v[pl.ds(p * ch, ch)] = coarse_all[:, p * ch : (p + 1) * ch]
     take_rows(coarse_v, me * coarse_out.shape[0], coarse_out)
-    later_all = jnp.concatenate([pre[p : p + n].reshape(total, ch) for p in range(3)], axis=1)
+    later_all = jnp.concatenate([pre[2 + p : 2 + p + n].reshape(total, ch) for p in range(3)], axis=1)
     lgr[...] = mm_nt(later_all, wc_flip).astype(BF).reshape(lgr.shape)
 
-    @pl.loop(1, n)
-    def _(k):
-        source = peer_of(k)
-        message(STK, stk_mine.at[0], stk_all.at[source], me, source).wait_recv()
+    all_blocks(STK, stk_all, n - 1).wait_recv()
 
     whole_v[0:wb, 0:ch] = (
         mm_tn(stk_all[...].reshape(total, wb), lgr[...].reshape(total, ch)) * scale
     )
     take_rows(whole_v.at[:, pl.ds(0, ch)], mine * down_out.shape[0], down_out)
 
-    @pl.loop(1, nb)
-    def _(k):
-        source = up_target(k)
-        message(UPS, up_mine.at[0], up_all.at[source // rep], me, source).wait_recv()
+    @pl.when(me < n - 1)
+    def _():
+        send_v().wait_send()
+
+    @pl.when(me > 0)
+    def _():
+        send_c().wait_send()
+        send_n().wait_send()
+
+    for buf, kind, shift in ((lat, LAT, 2), (cgr, CGR, 0)):
+        spread_near(buf, kind, me + shift, wait_send)
+        spread_rest(buf, kind, me + shift, wait_send)
+
+        @pl.loop(1, n // 2)
+        def _(k):
+            source = lax.rem(me + n - 2 * k, n)
+
+            @pl.when(jnp.logical_not(near_odd(buddy - source)))
+            def _():
+                forward(buf, kind, shift, source).wait_send()
+
+    all_blocks(DEP, dep_all, n - 1).wait_send()
+    all_blocks(STK, stk_all, n - 1).wait_send()
+    all_blocks(UPS, up_all, nb - 1).wait_recv()
 
     up_at = lax.rem(me * up_rows, block_rows)
     for b in range(nb):
         take_rows(up_all.at[b], up_at, up_out.at[:, pl.ds(b * wb, wb)])
 
-    @pl.when(me < n - 1)
-    def _():
-        send_v().wait_send()
-
-    @pl.when(me > 0)
-    def _():
-        send_c().wait_send()
-        send_n().wait_send()
-
-    for buf, kind, shift in ((lat, LAT, 2), (cgr, CGR, 0)):
-        spread(buf, kind, me + shift, wait_send)
-
-        @pl.loop(1, n // 2)
-        def _(k):
-            source = lax.rem(me + n - 2 * k, n)
-
-            @pl.when(jnp.logical_not(near_odd(buddy - source)))
-            def _():
-                forward(buf, kind, shift, source).wait_send()
-
-    @pl.loop(1, n)
-    def _(k):
-        block_send(DEP, dep_mine, dep_all, peer_of(k)).wait_send()
-        block_send(STK, stk_mine, stk_all, peer_of(k)).wait_send()
-
-    @pl.loop(1, nb)
-    def _(k):
-        up_send(up_target(k)).wait_send()
+    all_blocks(UPS, up_all, nb - 1).wait_send()
 
 
 def tail(*refs):
@@ -518,15 +580,18 @@
         pltpu.VMEM(levels.shape, jnp.int32),
         pltpu.VMEM((n + 5, cells, ch), BF), pltpu.VMEM((n + 3, cells, ch), BF),
         pltpu.VMEM((n, cells, ch), BF), pltpu.VMEM((n, cells, ch), F32),
-        pltpu.VMEM((n + 2, cells, ch), BF), pltpu.VMEM((n, cells, ch), BF),
+        pltpu.VMEM((n + 4, cells, ch), BF), pltpu.VMEM((n, cells, ch), BF),
         pltpu.VMEM((nb, cells, wb), BF), pltpu.VMEM((n, cells, wb), BF),
         pltpu.VMEM((nb, cells, wb), BF), pltpu.VMEM((n, cells, wb), BF),
         pltpu.VMEM((ch // block_rows, block_rows, wb), F32),
         pltpu.VMEM((nb, block_rows, wb), F32),
         pltpu.VMEM(wc.shape, F32), pltpu.VMEM((wb, ch), F32),
+        pltpu.VMEM((3, fine, ch), F32), pltpu.VMEM((3, fine, ch), F32),
         pltpu.SemaphoreType.DMA((3,)), pltpu.SemaphoreType.DMA((3,)),
-        pltpu.SemaphoreType.DMA((5, n)), pltpu.SemaphoreType.DMA((5, n)),
-        pltpu.SemaphoreType.DMA((2, n)), pltpu.SemaphoreType.DMA((13,)),
+        pltpu.SemaphoreType.DMA((2, n)), pltpu.SemaphoreType.DMA((2, n)),
+        pltpu.SemaphoreType.DMA((2, n)), pltpu.SemaphoreType.DMA((3,)),
+        pltpu.SemaphoreType.DMA((3,)), pltpu.SemaphoreType.DMA((13,)),
+        pltpu.SemaphoreType.REGULAR((n.bit_length() - 1,)),
     ]
     held = pl.pallas_call(
         functools.partial(kernel, n, scale),

time: 31.6 us -> 26.1 us (0.83)
  Pallas kernels: 30.8 us -> 25.3 us
    pallas_call x1, Pallas kernels: 30 us -> 24.5 us  [shards(): pl.pallas_call(functools.partial(kernel, n, scale), out_shape=tuple((pltp...]
where the time goes in v3:
time: 26.1 us; the launch traced here: 26 us
  Pallas kernels  25.3 us (97%)
  between operations  0.64 us (2%)
    pallas_call x1, Pallas kernels, shards(): pl.pallas_call(functools.partial(kernel, n, scale), out_shape=tuple((pltp...  24.5 us
    pallas_call x1, Pallas kernels, shards(): pl.pallas_call(tail, out_shape=tuple((jax.ShapeDtypeStruct(*result) for r...  0.8 us

profile of v3, /device:TPU:0, one launch (start us, length us, event | category | flops | bytes accessed | tf_op | source)
XLA Modules:
  0.0 26.0 jit_solution(8153051765389355671)
XLA Ops:
  0.6 24.5 %shard_map.128 = (bf16[2,12,8,256]{3,2,1,0:T(8,128)(2,1)S(1)}, bf16[1,6,4,256]{3,2,1,0:T(4,128)(2,1)S(1)}, f32[128,256]{1,0:T(8,128)S(1)}, f32[48,256]{1,0:T(8,128)S(1)}, f32[16,2048]{1,0:T(8,128)S(1)}) custom-call(bf16[2,12,8,256]{3,2,1,0:T(8,128)(2,1)} %vf.1, bf16[2,12,8,256]{3,2,1,0:T(8,128)(2,1)} %ct.1, bf16[6912,256]{1,0:T(8,128)(2,1)} %we.1, ...), custom_call_target="tpu_custom_call" | custom-call | tf_op jit(solution)/shard_map/pallas_call | solution.py:596
  25.2 0.8 %shard_map.129 = (bf16[2,12,8,256]{3,2,1,0:T(8,128)(2,1)}, bf16[1,6,4,256]{3,2,1,0:T(4,128)(2,1)}, f32[128,256]{1,0:T(8,128)}, f32[48,256]{1,0:T(8,128)}, f32[16,2048]{1,0:T(8,128)}) custom-call(bf16[2,12,8,256]{3,2,1,0:T(8,128)(2,1)S(1)} %get-tuple-element.10.refs_0_, bf16[1,6,4,256]{3,2,1,0:T(4,128)(2,1)S(1)} %get-tuple-element.11.refs_1_, ...), custom_call_target="tpu_custom_call" | custom-call | tf_op jit(solution)/shard_map/pallas_call | solution.py:604

commit v4 on v3

v4 whole, which is shorter than its diff:
```python
import functools
import math

import jax
import jax.numpy as jnp
import numpy as np
from jax import lax
from jax.experimental import pallas as pl
from jax.experimental.pallas import tpu as pltpu
from jax.sharding import PartitionSpec as P

two_pi = 2.0 * math.pi
BF = jnp.bfloat16
F32 = jnp.float32
MESH = pl.DeviceIdType.MESH

HALO_V, HALO_C, HALO_N = 0, 1, 2
LAT, CGR = 0, 1
BUDDY = 2
STK, DEP, UPS = 4, 5, 6

SINE = [(-1.0) ** k / math.factorial(2 * k + 1) for k in range(7)]
COSINE = [(-1.0) ** k / math.factorial(2 * k) for k in range(7)]

def mm(a, b):
    return jnp.dot(a, b, preferred_element_type=F32)


def mm_nt(a, b):
    return lax.dot_general(a, b, (((1,), (1,)), ((), ())), preferred_element_type=F32)


def mm_tn(a, b):
    return lax.dot_general(a, b, (((0,), (0,)), ((), ())), preferred_element_type=F32)


def half_turn(x):
    angle = (x - jnp.round(x)) * math.pi
    square = angle * angle
    sine, cosine = SINE[-1], COSINE[-1]
    for a, b in zip(SINE[-2::-1], COSINE[-2::-1]):
        sine = sine * square + a
        cosine = cosine * square + b
    return sine * angle, cosine


def depth_permutation(rows, cols):
    order = np.arange(2 * rows * cols).reshape(2, rows // 2, 2, cols // 2, 2)
    order = order.transpose(0, 2, 4, 1, 3).reshape(-1)
    picks = np.zeros((order.size, order.size), np.float32)
    picks[np.arange(order.size), order] = 1.0
    return picks


def kernel(
    n, scale, vf, ct, we, wd, wc, wu, wx, levels, perm,
    vg_out, code_out, down_out, coarse_out, up_out,
    vg_w, code_w, down_w, coarse_w, up_w, lat_turned,
    vbuf, cbuf, ebuf, we_v, wx_v, wd_v, wc_v, wu_v, perm_v, level_v,
    lat, cgr, near, cod, fac, pre, lgr, stk_mine, stk_all, dep_mine, dep_all, up_mine, up_all, up_wide, coarse_v, whole_v,
    acc_e, acc_d, hal_s, hal_r, msg_r, near_s, near_r, all_s, all_r, load_sem, out_sem, met,
):
    frames, rows, width, ch = vf.shape
    fine = frames * rows * width
    cells = fine // 8
    nb, _, wb = stk_mine.shape
    rep = n // nb
    me = lax.axis_index("tm")

    def peer_of(k):
        return lax.rem(me + k, n)

    odd = lax.rem(me, 2)
    buddy = me + 1 - 2 * odd
    other = me - 1 + 2 * odd
    has_other = (other >= 0) & (other < n)
    dims = n.bit_length() - 1

    def partner(d):
        return me + (1 - 2 * lax.rem(me // 2**d, 2)) * 2**d

    barrier = pltpu.get_barrier_semaphore()
    for d in range(dims):
        pl.semaphore_signal(barrier, inc=1, device_id={"tm": partner(d)}, device_id_type=MESH)

    @pl.when(has_other)
    def _():
        pl.semaphore_signal(barrier, inc=1, device_id={"tm": other}, device_id_type=MESH)

    def tell(d):
        if d < dims:
            pl.semaphore_signal(
                met.at[d], inc=1, device_id={"tm": partner(d)}, device_id_type=MESH
            )

    def hear(d):
        if d < dims:
            pl.semaphore_wait(met.at[d], 1)

    inner = pl.ds(1, rows)
    third = we.shape[0] // 3
    loads = [
        pltpu.make_async_copy(vf, vbuf.at[2:4, inner], load_sem.at[0]),
        pltpu.make_async_copy(ct, cbuf.at[0:2, inner], load_sem.at[1]),
    ]
    for k, (at, count) in enumerate(((2 * third, third), (0, 2 * third))):
        span = pl.ds(at, count)
        loads.append(pltpu.make_async_copy(we.at[span], we_v.at[span], load_sem.at[2 + 2 * k]))
        loads.append(pltpu.make_async_copy(wx.at[span], wx_v.at[span], load_sem.at[3 + 2 * k]))
    small = [
        pltpu.make_async_copy(src, dst, load_sem.at[6 + k])
        for k, (src, dst) in enumerate(
            ((perm, perm_v), (wd, wd_v), (wu, wu_v), (wc, wc_v), (levels, level_v))
        )
    ]
    for load in loads + small:
        load.start()

    def halo(kind, src, dst, peer):
        return pltpu.make_async_remote_copy(
            src_ref=src, dst_ref=dst, send_sem=hal_s.at[kind], recv_sem=hal_r.at[kind],
            device_id={"tm": peer}, device_id_type=MESH,
        )

    def block(kind, src, dst, peer, receives=None, sends=None):
        return pltpu.make_async_remote_copy(
            src_ref=src, dst_ref=dst,
            send_sem=all_s.at[kind] if sends is None else sends,
            recv_sem=all_r.at[kind] if receives is None else receives,
            device_id={"tm": peer}, device_id_type=MESH,
        )

    def all_blocks(kind, buf, count):
        return block(kind, buf.at[pl.ds(0, count)], buf.at[pl.ds(0, count)], buddy)

    def send_v():
        return halo(HALO_V, vf, vbuf.at[0:2, inner], me + 1)

    def send_c():
        return halo(HALO_C, ct, cbuf.at[2:4, inner], me - 1)

    def send_n():
        return halo(HALO_N, vf, vbuf.at[4:6, inner], me - 1)

    for buf in (vbuf, cbuf, ebuf):
        edge = jnp.zeros((buf.shape[0], 1, width, ch), BF)
        buf[:, 0:1] = edge
        buf[:, rows + 1 : rows + 2] = edge
    blank = jnp.zeros((2, rows, width, ch), BF)

    @pl.when(me == 0)
    def _():
        vbuf[0:2, 1 : rows + 1] = blank

    @pl.when(me == n - 1)
    def _():
        cbuf[2:4, 1 : rows + 1] = blank
        vbuf[4:6, 1 : rows + 1] = blank

    lat[0:2] = jnp.zeros((2, cells, ch), BF)
    lat[n + 2 : n + 5] = jnp.zeros((3, cells, ch), BF)
    for k in (1, 2, 3):
        @pl.when(me + k >= n)
        def _():
            near[k - 1] = jnp.zeros((cells, ch), BF)

    fac[n : n + 3] = jnp.zeros((3, cells, ch), F32)
    pre[0:2] = jnp.zeros((2, cells, ch), BF)
    pre[n + 2 : n + 4] = jnp.zeros((2, cells, ch), BF)

    pl.semaphore_wait(barrier, jnp.where(has_other, dims + 1, dims))
    tell(0)

    @pl.when(me < n - 1)
    def _():
        send_v().start()

    @pl.when(me > 0)
    def _():
        send_c().start()
        send_n().start()

    def taps(buf, at):
        return jnp.concatenate(
            [buf[at : at + 2, q : q + rows].reshape(fine, ch) for q in range(3)], axis=1
        )

    def past(buf, at, weight, parts):
        left = jnp.concatenate([taps(buf, at + p) for p in parts], axis=1)
        out = []
        for r in range(3):
            right = jnp.concatenate(
                [
                    weight[pl.ds(((3 * p + q) * 3 + r) * ch, ch)]
                    for p in parts
                    for q in range(3)
                ],
                axis=0,
            )
            out.append(mm(left, right))
        return out

    def future(buf, at, weight, parts):
        left = jnp.concatenate([taps(buf, at + p) for p in parts], axis=1)
        out = []
        for r in range(3):
            right = jnp.concatenate(
                [
                    weight[pl.ds((((2 - p) * 3 + 2 - q) * 3 + 2 - r) * ch, ch)]
                    for p in parts
                    for q in range(3)
                ],
                axis=1,
            )
            out.append(mm_nt(left, right))
        return out

    def keep(acc, parts):
        for r in range(3):
            acc[r] = parts[r]

    def added(acc, parts):
        return [acc[r] + parts[r] for r in range(3)]

    lane = lax.broadcasted_iota(jnp.int32, (fine // width, width, ch), 1)

    def aligned(parts):
        a, b, c = [x.reshape(fine // width, width, ch) for x in parts]
        a = jnp.where(lane == 0, 0.0, pltpu.roll(a, 1, 1))
        c = jnp.where(lane == width - 1, 0.0, pltpu.roll(c, width - 1, 1))
        return (a + b + c).reshape(fine, ch)

    hear(0)
    tell(1)

    loads[0].wait()
    loads[2].wait()
    keep(acc_e, past(vbuf, 0, we_v, (2,)))
    hear(1)
    tell(2)
    loads[1].wait()
    loads[3].wait()
    keep(acc_d, future(cbuf, 0, wx_v, (0,)))
    hear(2)
    tell(3)
    loads[4].wait()

    @pl.when(me > 0)
    def _():
        send_v().wait_recv()

    enc = added(acc_e, past(vbuf, 0, we_v, (1, 0)))
    pre_enc = aligned(enc)
    sig = jax.nn.sigmoid(pre_enc)
    own = vbuf[2:4, 1 : rows + 1].reshape(fine, ch).astype(F32)
    hidden = (own + pre_enc * sig).astype(BF)

    def slope_of(x, s):
        return s * (1.0 + x * (1.0 - s))

    for load in small:
        load.wait()

    def regroup(field, store):
        moved = mm(perm_v[0], field)
        blocks = [moved[b * cells : (b + 1) * cells].astype(BF) for b in range(8)]
        per = nb // 8
        for b in range(8):
            for h in range(per):
                store[b * per + h] = blocks[b][:, h * wb : (h + 1) * wb]
        return jnp.concatenate(blocks, axis=1)

    half_n = n // 2

    def parity_send(buf, kind, slot, k):
        peer = lax.rem(me + 2 * k, n)
        return block(kind, buf.at[slot], buf.at[slot], peer, msg_r.at[kind, me // 2])

    def buddy_send(buf, kind, slot):
        return block(BUDDY + kind, buf.at[slot], buf.at[slot], buddy)

    def near_send(k):
        return block(
            CGR, cgr.at[me], near.at[k - 1], me - k, near_r.at[k - 1], near_s.at[k - 1]
        )

    def arrival(buf, kind, slot, source):
        return block(kind, buf.at[slot], buf.at[slot], buddy, msg_r.at[kind, source // 2])

    def inside(k):
        return (me + k >= 0) & (me + k < n)

    def spread(buf, kind, slot):
        buddy_send(buf, kind, slot).start()

        @pl.loop(1, half_n)
        def _(k):
            parity_send(buf, kind, slot, k).start()

    def relay(buf, kind, shift):
        @pl.loop(1, half_n)
        def _(k):
            source = lax.rem(me + n - 2 * k, n)
            slot = source + shift
            arrival(buf, kind, slot, source).wait_recv()
            block(BUDDY + kind, buf.at[slot], buf.at[slot], buddy).start()

    lat[me + 2] = mm(regroup(hidden, stk_mine), wd_v[...]).astype(BF)
    hear(3)
    for d in range(4, dims):
        tell(d)
        hear(d)
    spread(lat, LAT, me + 2)

    loads[5].wait()

    @pl.when(me < n - 1)
    def _():
        send_c().wait_recv()

    dec = added(acc_d, future(cbuf, 0, wx_v, (1, 2)))
    own_c = cbuf[0:2, 1 : rows + 1].reshape(fine, ch).astype(F32)
    depth = regroup((own_c + aligned(dec)).astype(BF), dep_mine)

    def block_send(kind, mine, everyone, peer):
        return block(kind, mine.at[peer // rep], everyone.at[me], peer)

    @pl.loop(1, n)
    def _(k):
        block_send(DEP, dep_mine, dep_all, peer_of(k)).start()

    cgr[me] = mm_nt(depth, wu_v[...]).astype(BF)

    for k in (1, 2, 3):
        @pl.when(inside(-k))
        def _():
            near_send(k).start()

    spread(cgr, CGR, me)

    dep_all[me] = dep_mine[me // rep]
    stk_all[me] = stk_mine[me // rep]

    def give(src, dst, k):
        return pltpu.make_async_copy(src, dst, out_sem.at[k])

    half = ((level_v[...].astype(F32) - 1.0) * 0.5).reshape(1, ch)
    inverse = 1.0 / half

    def coder(frame, count):
        columns = jnp.concatenate(
            [lat[pl.ds(frame + p, count)].reshape(count * cells, ch) for p in range(3)], axis=1
        )
        squashed = jnp.tanh(mm(columns, wc_v[...]))
        bounded = half * squashed
        sine, cosine = half_turn(bounded)
        codes = ((bounded - sine * cosine * (2.0 / two_pi)) * inverse).astype(BF)
        return codes, (2.0 * sine * sine) * (1.0 - squashed * squashed)

    wc_flip = jnp.concatenate([wc_v[pl.ds((2 - p) * ch, ch)] for p in range(3)], axis=1)

    @pl.when(me < n - 1)
    def _():
        send_n().wait_recv()

    ahead = aligned(past(vbuf, 2, we_v, (0, 1, 2)))

    relay(lat, LAT, 2)

    @pl.loop(1, n)
    def _(k):
        block_send(STK, stk_mine, stk_all, peer_of(k)).start()

    def moved(perm, x):
        high = x.astype(BF)
        rest = (x - high.astype(F32)).astype(BF)
        return mm(perm, high) + mm(perm, rest)

    slopes = [
        moved(perm_v[0], slope_of(x, s))
        for x, s in ((pre_enc, sig), (ahead, jax.nn.sigmoid(ahead)))
    ]

    all_blocks(BUDDY + LAT, lat, half_n).wait_recv()
    step = min(n, 16)
    total = n * cells

    @pl.loop(0, n // step)
    def _(k):
        at = k * step
        codes, factor = coder(at, step)
        cod[pl.ds(at, step)] = codes.reshape(step, cells, ch)
        fac[pl.ds(at, step)] = factor.reshape(step, cells, ch)

    code_w[...] = cod[me].reshape(code_w.shape)
    code_out_copy = give(code_w, code_out, 0)
    code_out_copy.start()
    codes_turned = cod[...].reshape(total, ch).T
    lat_turned[...] = lat[0 : n + 2].reshape((n + 2) * cells, ch).T

    all_blocks(DEP, dep_all, n - 1).wait_recv()

    up_part = mm(codes_turned, dep_all[...].reshape(total, wb)) * scale
    block_rows = up_mine.shape[1]
    up_mine[...] = up_part.astype(BF).reshape(up_mine.shape)
    up_rows = ch // n
    mine = lax.rem(me, rep)
    my_block = me // rep

    def up_target(k):
        return mine + rep * lax.rem(my_block + k, nb)

    direct = block_rows == up_rows
    blocks_in = up_out if direct else up_all

    def up_send(peer):
        return block(UPS, up_mine.at[peer * up_rows // block_rows], blocks_in.at[my_block], peer)

    @pl.loop(1, nb)
    def _(k):
        up_send(up_target(k)).start()

    own_copy = give(up_mine.at[me * up_rows // block_rows], blocks_in.at[my_block], 4)
    own_copy.start()

    def take_rows(buf, at, out):
        count = out.shape[0]
        if count % 8 == 0:
            out[...] = buf[pl.ds(pl.multiple_of(at, 8), count)]
        else:
            for k in range(count):
                out[pl.ds(k, 1)] = buf[pl.ds(at + k, 1)]

    for k in (1, 2, 3):
        @pl.when(inside(k))
        def _():
            near_send(k).wait_recv()

    near_grads = jnp.concatenate([cgr[me], *[near[k] for k in range(3)]], axis=0).astype(F32)
    ahead_grad = near_grads * fac[pl.ds(me, 4)].reshape(4 * cells, ch)
    later = jnp.concatenate(
        [ahead_grad[p * cells : (p + 2) * cells].astype(BF) for p in range(3)], axis=1
    )
    grad_lat = mm_nt(later, wc_flip).astype(BF)

    deep_grad = mm_nt(grad_lat, wd_v[...])
    deep_rows = [
        jnp.concatenate(
            [
                deep_grad[frame * cells : (frame + 1) * cells, b * ch : (b + 1) * ch]
                for b in range(8)
            ],
            axis=0,
        )
        for frame in range(2)
    ]
    back = perm_v[1]
    for frame in range(2):
        ebuf[2 * frame : 2 * frame + 2, 1 : rows + 1] = (
            mm(back, (deep_rows[frame] * slopes[frame]).astype(BF))
            .astype(BF)
            .reshape(2, rows, width, ch)
        )
    hidden_grad = moved(back, deep_rows[0])

    bck = future(ebuf, 0, we_v, (0, 1, 2))
    vg_w[...] = (hidden_grad + aligned(bck)).astype(BF).reshape(vg_w.shape)
    vg_copy = give(vg_w, vg_out, 1)
    vg_copy.start()
    relay(cgr, CGR, 0)
    all_blocks(BUDDY + CGR, cgr, half_n).wait_recv()
    pre[2 : n + 2] = (cgr[0:n].astype(F32) * fac[0:n]).astype(BF)
    long = (n + 2) * cells
    coarse_rows = coarse_w.shape[0]
    piece = math.gcd(coarse_rows, ch)
    if piece % 16 == 0:
        for k in range(coarse_rows // piece):
            at = me * coarse_rows + k * piece
            left = lat_turned[pl.ds(pl.multiple_of(lax.rem(at, ch), piece), piece)]
            right = pre[pl.ds(2 - at // ch, n + 2)].reshape(long, ch)
            coarse_w[k * piece : (k + 1) * piece] = mm(left, right) * scale
    else:
        for p in range(3):
            coarse_v[pl.ds(p * ch, ch)] = (
                mm(lat_turned[...], pre[2 - p : 2 - p + n + 2].reshape(long, ch)) * scale
            )
        take_rows(coarse_v, me * coarse_rows, coarse_w)
    coarse_copy = give(coarse_w, coarse_out, 2)
    coarse_copy.start()
    later_all = jnp.concatenate([pre[2 + p : 2 + p + n].reshape(total, ch) for p in range(3)], axis=1)
    lgr[...] = mm_nt(later_all, wc_flip).astype(BF).reshape(lgr.shape)

    all_blocks(STK, stk_all, n - 1).wait_recv()

    whole_v[...] = (
        mm_tn(stk_all[...].reshape(total, wb), lgr[...].reshape(total, ch)) * scale
    )
    take_rows(whole_v, mine * down_out.shape[0], down_w)
    down_copy = give(down_w, down_out, 3)
    down_copy.start()

    @pl.when(me < n - 1)
    def _():
        send_v().wait_send()

    @pl.when(me > 0)
    def _():
        send_c().wait_send()
        send_n().wait_send()

    all_blocks(LAT, lat, half_n - 1).wait_send()
    all_blocks(CGR, cgr, half_n - 1).wait_send()
    all_blocks(BUDDY + LAT, lat, half_n).wait_send()
    all_blocks(BUDDY + CGR, cgr, half_n).wait_send()
    for k in (1, 2, 3):
        @pl.when(inside(-k))
        def _():
            near_send(k).wait_send()

    all_blocks(DEP, dep_all, n - 1).wait_send()
    all_blocks(STK, stk_all, n - 1).wait_send()
    for copy in (code_out_copy, vg_copy, coarse_copy, down_copy, own_copy):
        copy.wait()
    all_blocks(UPS, blocks_in, nb - 1).wait_recv()
    all_blocks(UPS, blocks_in, nb - 1).wait_send()
    if not direct:
        up_wide[...] = up_all[...].astype(F32)
        for b in range(nb):
            take_rows(up_wide.at[b], lax.rem(me * up_rows, block_rows), up_w.at[b])
        up_copy = give(up_w, up_out, 0)
        up_copy.start()
        up_copy.wait()


def tail(vg, code, down, coarse, up, vg_out, code_out, down_out, coarse_out, up_out, wide, sems):
    nb, _, wb = up.shape
    pairs = ((vg, vg_out), (code, code_out), (down, down_out), (coarse, coarse_out), (wide, up_out))
    copies = [pltpu.make_async_copy(src, dst, sems.at[k]) for k, (src, dst) in enumerate(pairs)]
    for copy in copies[:4]:
        copy.start()
    for b in range(nb):
        wide[:, b * wb : (b + 1) * wb] = up[b].astype(F32)
    copies[4].start()
    for copy in copies:
        copy.wait()


def shards(n, vf, ct, we, wd, wc, wu, wx, levels):
    frames, rows, width, ch = vf.shape
    deep = wd.shape[0]
    fine = frames * rows * width
    cells = fine // 8
    wb = max(128, deep // n)
    nb = deep // wb
    up_rows = ch // n
    block_rows = max(8, up_rows)
    scale = 1.0 / math.sqrt(n * fine)
    picks = depth_permutation(rows, width)
    perm = jnp.asarray(np.stack([picks, picks.T]), BF)
    anywhere = pl.BlockSpec(memory_space=pl.ANY)
    results = (
        (vf.shape, BF),
        ((frames // 2, rows // 2, width // 2, ch), BF),
        ((deep // n, ch), F32),
        ((wc.shape[0] // n, ch), F32),
        ((up_rows, deep), F32),
    )
    four = (4, rows + 2, width, ch)
    held_shapes = (
        results[0],
        results[1],
        results[2],
        results[3],
        ((nb, up_rows, wb), BF if block_rows == up_rows else F32),
    )
    scratch = [
        pltpu.VMEM(vf.shape, BF), pltpu.VMEM(results[1][0], BF), pltpu.VMEM(results[2][0], F32), pltpu.VMEM(results[3][0], F32),
        pltpu.VMEM((nb, up_rows, wb), F32), pltpu.VMEM((ch, (n + 2) * cells), BF),
        pltpu.VMEM((6, rows + 2, width, ch), BF), pltpu.VMEM(four, BF), pltpu.VMEM(four, BF),
        pltpu.VMEM(we.shape, BF), pltpu.VMEM(wx.shape, BF), pltpu.VMEM(wd.shape, BF),
        pltpu.VMEM(wc.shape, BF), pltpu.VMEM(wu.shape, BF), pltpu.VMEM(perm.shape, BF),
        pltpu.VMEM(levels.shape, jnp.int32),
        pltpu.VMEM((n + 5, cells, ch), BF), pltpu.VMEM((n, cells, ch), BF), pltpu.VMEM((3, cells, ch), BF),
        pltpu.VMEM((n, cells, ch), BF), pltpu.VMEM((n + 3, cells, ch), F32),
        pltpu.VMEM((n + 4, cells, ch), BF), pltpu.VMEM((n, cells, ch), BF),
        pltpu.VMEM((nb, cells, wb), BF), pltpu.VMEM((n, cells, wb), BF),
        pltpu.VMEM((nb, cells, wb), BF), pltpu.VMEM((n, cells, wb), BF),
        pltpu.VMEM((ch // block_rows, block_rows, wb), BF),
        pltpu.VMEM((nb, block_rows, wb), BF), pltpu.VMEM((nb, block_rows, wb), F32),
        pltpu.VMEM(wc.shape, F32), pltpu.VMEM((wb, ch), F32),
        pltpu.VMEM((3, fine, ch), F32), pltpu.VMEM((3, fine, ch), F32),
        pltpu.SemaphoreType.DMA((3,)), pltpu.SemaphoreType.DMA((3,)),
        pltpu.SemaphoreType.DMA((2, n // 2)), pltpu.SemaphoreType.DMA((3,)),
        pltpu.SemaphoreType.DMA((3,)), pltpu.SemaphoreType.DMA((7,)),
        pltpu.SemaphoreType.DMA((7,)), pltpu.SemaphoreType.DMA((11,)),
        pltpu.SemaphoreType.DMA((5,)),
        pltpu.SemaphoreType.REGULAR((n.bit_length() - 1,)),
    ]
    held = pl.pallas_call(
        functools.partial(kernel, n, scale),
        out_shape=tuple(pltpu.VMEM(*shape) for shape in held_shapes),
        in_specs=[anywhere] * 9,
        out_specs=(anywhere,) * 5,
        scratch_shapes=scratch,
        compiler_params=pltpu.CompilerParams(collective_id=0, has_side_effects=True),
    )(vf, ct, we, wd, wc, wu, wx, levels, perm)
    return pl.pallas_call(
        tail,
        out_shape=tuple(jax.ShapeDtypeStruct(*result) for result in results),
        in_specs=[anywhere] * 4 + [pl.BlockSpec(memory_space=pltpu.VMEM)],
        out_specs=(anywhere,) * 5,
        scratch_shapes=[pltpu.VMEM((up_rows, deep), F32), pltpu.SemaphoreType.DMA((5,))],
    )(*[pltpu.with_memory_space_constraint(part, pltpu.VMEM) for part in held])


def solution(mesh):
    placed = (P("tm", "grp", None, None), P("tm", "grp", None, None), P(), P(), P(), P(), P(), P())
    return jax.shard_map(
        functools.partial(shards, mesh.shape["tm"]),
        mesh=mesh,
        in_specs=placed,
        out_specs=(
            P("tm", "grp", None, None),
            P("tm", "grp", None, None),
            P(("grp", "tm"), None),
            P(("grp", "tm"), None),
            P(("grp", "tm"), None),
        ),
        check_vma=False,
    )
```

time: 26.1 us -> 24 us (0.920)
  Pallas kernels: 25.3 us -> 23.2 us
    pallas_call x1, Pallas kernels: 24.5 us -> 22.4 us  [shards(): pl.pallas_call(functools.partial(kernel, n, scale), out_shape=tuple((pltp...]
where the time goes in v4:
time: 24 us; the launch traced here: 23.9 us
  Pallas kernels  23.2 us (97%)
  between operations  0.64 us (3%)
    pallas_call x1, Pallas kernels, shards(): pl.pallas_call(functools.partial(kernel, n, scale), out_shape=tuple((pltp...  22.4 us
    pallas_call x1, Pallas kernels, shards(): pl.pallas_call(tail, out_shape=tuple((jax.ShapeDtypeStruct(*result) for r...  0.8 us

profile of v4, /device:TPU:0, one launch (start us, length us, event | category | flops | bytes accessed | tf_op | source)
XLA Modules:
  0.0 23.9 jit_solution(13189911626481472780)
XLA Ops:
  0.6 22.4 %shard_map.128 = (bf16[2,12,8,256]{3,2,1,0:T(8,128)(2,1)S(1)}, bf16[1,6,4,256]{3,2,1,0:T(4,128)(2,1)S(1)}, f32[128,256]{1,0:T(8,128)S(1)}, f32[48,256]{1,0:T(8,128)S(1)}, bf16[16,16,128]{2,1,0:T(8,128)(2,1)S(1)}) custom-call(bf16[2,12,8,256]{3,2,1,0:T(8,128)(2,1)} %vf.1, bf16[2,12,8,256]{3,2,1,0:T(8,128)(2,1)} %ct.1, bf16[6912,256]{1,0:T(8,128)(2,1)} %we.1, ...), custom_call_target="tpu_custom_call" | custom-call | tf_op jit(solution)/shard_map/pallas_call | solution.py:599
  23.1 0.8 %shard_map.129 = (bf16[2,12,8,256]{3,2,1,0:T(8,128)(2,1)}, bf16[1,6,4,256]{3,2,1,0:T(4,128)(2,1)}, f32[128,256]{1,0:T(8,128)}, f32[48,256]{1,0:T(8,128)}, f32[16,2048]{1,0:T(8,128)}) custom-call(bf16[2,12,8,256]{3,2,1,0:T(8,128)(2,1)S(1)} %get-tuple-element.10.vg, bf16[1,6,4,256]{3,2,1,0:T(4,128)(2,1)S(1)} %get-tuple-element.11.code, ...), custom_call_target="tpu_custom_call" | custom-call | tf_op jit(solution)/shard_map/pallas_call | solution.py:607

commit v5 on v4

--- a/solution.py
+++ b/solution.py
@@ -134,7 +134,7 @@
         return block(kind, buf.at[pl.ds(0, count)], buf.at[pl.ds(0, count)], buddy)
 
     def send_v():
-        return halo(HALO_V, vf, vbuf.at[0:2, inner], me + 1)
+        return halo(HALO_V, vbuf.at[2:4, inner], vbuf.at[0:2, inner], me + 1)
 
     def send_c():
         return halo(HALO_C, ct, cbuf.at[2:4, inner], me - 1)
@@ -170,6 +170,8 @@
 
     pl.semaphore_wait(barrier, jnp.where(has_other, dims + 1, dims))
     tell(0)
+
+    loads[0].wait()
 
     @pl.when(me < n - 1)
     def _():
@@ -233,7 +235,6 @@
     hear(0)
     tell(1)
 
-    loads[0].wait()
     loads[2].wait()
     keep(acc_e, past(vbuf, 0, we_v, (2,)))
     hear(1)

time: 24 us -> 23.8 us (level)
  no operation moved by 1% of the time
where the time goes in v5:
time: 23.8 us; the launch traced here: 23.6 us
  Pallas kernels  23 us (97%)
  between operations  0.64 us (3%)
    pallas_call x1, Pallas kernels, shards(): pl.pallas_call(functools.partial(kernel, n, scale), out_shape=tuple((pltp...  22.2 us
    pallas_call x1, Pallas kernels, shards(): pl.pallas_call(tail, out_shape=tuple((jax.ShapeDtypeStruct(*result) for r...  0.8 us

profile of v5, /device:TPU:0, one launch (start us, length us, event | category | flops | bytes accessed | tf_op | source)
XLA Modules:
  0.0 23.6 jit_solution(12485363826866458309)
XLA Ops:
  0.6 22.2 %shard_map.128 = (bf16[2,12,8,256]{3,2,1,0:T(8,128)(2,1)S(1)}, bf16[1,6,4,256]{3,2,1,0:T(4,128)(2,1)S(1)}, f32[128,256]{1,0:T(8,128)S(1)}, f32[48,256]{1,0:T(8,128)S(1)}, bf16[16,16,128]{2,1,0:T(8,128)(2,1)S(1)}) custom-call(bf16[2,12,8,256]{3,2,1,0:T(8,128)(2,1)} %vf.1, bf16[2,12,8,256]{3,2,1,0:T(8,128)(2,1)} %ct.1, bf16[6912,256]{1,0:T(8,128)(2,1)} %we.1, ...), custom_call_target="tpu_custom_call" | custom-call | tf_op jit(solution)/shard_map/pallas_call | solution.py:600
  22.8 0.8 %shard_map.129 = (bf16[2,12,8,256]{3,2,1,0:T(8,128)(2,1)}, bf16[1,6,4,256]{3,2,1,0:T(4,128)(2,1)}, f32[128,256]{1,0:T(8,128)}, f32[48,256]{1,0:T(8,128)}, f32[16,2048]{1,0:T(8,128)}) custom-call(bf16[2,12,8,256]{3,2,1,0:T(8,128)(2,1)S(1)} %get-tuple-element.10.vg, bf16[1,6,4,256]{3,2,1,0:T(4,128)(2,1)S(1)} %get-tuple-element.11.code, ...), custom_call_target="tpu_custom_call" | custom-call | tf_op jit(solution)/shard_map/pallas_call | solution.py:608

commit v6 on v5

--- a/solution.py
+++ b/solution.py
@@ -14,7 +14,7 @@
 F32 = jnp.float32
 MESH = pl.DeviceIdType.MESH
 
-HALO_V, HALO_C, HALO_N = 0, 1, 2
+HALO_V, HALO_C, HALO_N, HALO_W = 0, 1, 2, 3
 LAT, CGR = 0, 1
 BUDDY = 2
 STK, DEP, UPS = 4, 5, 6
@@ -134,7 +134,10 @@
         return block(kind, buf.at[pl.ds(0, count)], buf.at[pl.ds(0, count)], buddy)
 
     def send_v():
-        return halo(HALO_V, vbuf.at[2:4, inner], vbuf.at[0:2, inner], me + 1)
+        return halo(HALO_V, vbuf.at[3:4, inner], vbuf.at[1:2, inner], me + 1)
+
+    def send_w():
+        return halo(HALO_W, vbuf.at[2:3, inner], vbuf.at[0:1, inner], me + 1)
 
     def send_c():
         return halo(HALO_C, ct, cbuf.at[2:4, inner], me - 1)
@@ -176,6 +179,7 @@
     @pl.when(me < n - 1)
     def _():
         send_v().start()
+        send_w().start()
 
     @pl.when(me > 0)
     def _():
@@ -250,7 +254,13 @@
     def _():
         send_v().wait_recv()
 
-    enc = added(acc_e, past(vbuf, 0, we_v, (1, 0)))
+    keep(acc_e, added(acc_e, past(vbuf, 0, we_v, (1,))))
+
+    @pl.when(me > 0)
+    def _():
+        send_w().wait_recv()
+
+    enc = added(acc_e, past(vbuf, 0, we_v, (0,)))
     pre_enc = aligned(enc)
     sig = jax.nn.sigmoid(pre_enc)
     own = vbuf[2:4, 1 : rows + 1].reshape(fine, ch).astype(F32)
@@ -503,6 +513,7 @@
     @pl.when(me < n - 1)
     def _():
         send_v().wait_send()
+        send_w().wait_send()
 
     @pl.when(me > 0)
     def _():
@@ -590,7 +601,7 @@
         pltpu.VMEM((nb, block_rows, wb), BF), pltpu.VMEM((nb, block_rows, wb), F32),
         pltpu.VMEM(wc.shape, F32), pltpu.VMEM((wb, ch), F32),
         pltpu.VMEM((3, fine, ch), F32), pltpu.VMEM((3, fine, ch), F32),
-        pltpu.SemaphoreType.DMA((3,)), pltpu.SemaphoreType.DMA((3,)),
+        pltpu.SemaphoreType.DMA((4,)), pltpu.SemaphoreType.DMA((4,)),
         pltpu.SemaphoreType.DMA((2, n // 2)), pltpu.SemaphoreType.DMA((3,)),
         pltpu.SemaphoreType.DMA((3,)), pltpu.SemaphoreType.DMA((7,)),
         pltpu.SemaphoreType.DMA((7,)), pltpu.SemaphoreType.DMA((11,)),

time: 23.8 us -> 23.4 us (0.983)
  Pallas kernels: 23 us -> 22.6 us
    pallas_call x1, Pallas kernels: 22.2 us -> 21.8 us  [shards(): pl.pallas_call(functools.partial(kernel, n, scale), out_shape=tuple((pltp...]
where the time goes in v6:
time: 23.4 us; the launch traced here: 23.3 us
  Pallas kernels  22.6 us (97%)
  between operations  0.64 us (3%)
    pallas_call x1, Pallas kernels, shards(): pl.pallas_call(functools.partial(kernel, n, scale), out_shape=tuple((pltp...  21.8 us
    pallas_call x1, Pallas kernels, shards(): pl.pallas_call(tail, out_shape=tuple((jax.ShapeDtypeStruct(*result) for r...  0.8 us

profile of v6, /device:TPU:0, one launch (start us, length us, event | category | flops | bytes accessed | tf_op | source)
XLA Modules:
  0.0 23.3 jit_solution(9457639887109996889)
XLA Ops:
  0.6 21.8 %shard_map.128 = (bf16[2,12,8,256]{3,2,1,0:T(8,128)(2,1)S(1)}, bf16[1,6,4,256]{3,2,1,0:T(4,128)(2,1)S(1)}, f32[128,256]{1,0:T(8,128)S(1)}, f32[48,256]{1,0:T(8,128)S(1)}, bf16[16,16,128]{2,1,0:T(8,128)(2,1)S(1)}) custom-call(bf16[2,12,8,256]{3,2,1,0:T(8,128)(2,1)} %vf.1, bf16[2,12,8,256]{3,2,1,0:T(8,128)(2,1)} %ct.1, bf16[6912,256]{1,0:T(8,128)(2,1)} %we.1, ...), custom_call_target="tpu_custom_call" | custom-call | tf_op jit(solution)/shard_map/pallas_call | solution.py:611
  22.5 0.8 %shard_map.129 = (bf16[2,12,8,256]{3,2,1,0:T(8,128)(2,1)}, bf16[1,6,4,256]{3,2,1,0:T(4,128)(2,1)}, f32[128,256]{1,0:T(8,128)}, f32[48,256]{1,0:T(8,128)}, f32[16,2048]{1,0:T(8,128)}) custom-call(bf16[2,12,8,256]{3,2,1,0:T(8,128)(2,1)S(1)} %get-tuple-element.10.vg, bf16[1,6,4,256]{3,2,1,0:T(4,128)(2,1)S(1)} %get-tuple-element.11.code, ...), custom_call_target="tpu_custom_call" | custom-call | tf_op jit(solution)/shard_map/pallas_call | solution.py:619

commit v7 on v6

--- a/solution.py
+++ b/solution.py
@@ -55,7 +55,7 @@
 def kernel(
     n, scale, vf, ct, we, wd, wc, wu, wx, levels, perm,
     vg_out, code_out, down_out, coarse_out, up_out,
-    vg_w, code_w, down_w, coarse_w, up_w, lat_turned,
+    vg_w, code_w, down_w, coarse_w, up_w, lat_turned, wd_t, wc_t,
     vbuf, cbuf, ebuf, we_v, wx_v, wd_v, wc_v, wu_v, perm_v, level_v,
     lat, cgr, near, cod, fac, pre, lgr, stk_mine, stk_all, dep_mine, dep_all, up_mine, up_all, up_wide, coarse_v, whole_v,
     acc_e, acc_d, hal_s, hal_r, msg_r, near_s, near_r, all_s, all_r, load_sem, out_sem, met,
@@ -240,14 +240,14 @@
     tell(1)
 
     loads[2].wait()
-    keep(acc_e, past(vbuf, 0, we_v, (2,)))
     hear(1)
     tell(2)
+    keep(acc_e, past(vbuf, 0, we_v, (2,)))
+    hear(2)
+    tell(3)
     loads[1].wait()
     loads[3].wait()
     keep(acc_d, future(cbuf, 0, wx_v, (0,)))
-    hear(2)
-    tell(3)
     loads[4].wait()
 
     @pl.when(me > 0)
@@ -368,8 +368,6 @@
         codes = ((bounded - sine * cosine * (2.0 / two_pi)) * inverse).astype(BF)
         return codes, (2.0 * sine * sine) * (1.0 - squashed * squashed)
 
-    wc_flip = jnp.concatenate([wc_v[pl.ds((2 - p) * ch, ch)] for p in range(3)], axis=1)
-
     @pl.when(me < n - 1)
     def _():
         send_n().wait_recv()
@@ -391,6 +389,10 @@
         moved(perm_v[0], slope_of(x, s))
         for x, s in ((pre_enc, sig), (ahead, jax.nn.sigmoid(ahead)))
     ]
+
+    wd_t[...] = wd_v[...].T
+    for p in range(3):
+        wc_t[p * ch : (p + 1) * ch] = wc_v[(2 - p) * ch : (3 - p) * ch].T
 
     all_blocks(BUDDY + LAT, lat, half_n).wait_recv()
     step = min(n, 16)
@@ -452,9 +454,9 @@
     later = jnp.concatenate(
         [ahead_grad[p * cells : (p + 2) * cells].astype(BF) for p in range(3)], axis=1
     )
-    grad_lat = mm_nt(later, wc_flip).astype(BF)
-
-    deep_grad = mm_nt(grad_lat, wd_v[...])
+    grad_lat = mm(later, wc_t[...]).astype(BF)
+
+    deep_grad = mm(grad_lat, wd_t[...])
     deep_rows = [
         jnp.concatenate(
             [
@@ -499,7 +501,7 @@
     coarse_copy = give(coarse_w, coarse_out, 2)
     coarse_copy.start()
     later_all = jnp.concatenate([pre[2 + p : 2 + p + n].reshape(total, ch) for p in range(3)], axis=1)
-    lgr[...] = mm_nt(later_all, wc_flip).astype(BF).reshape(lgr.shape)
+    lgr[...] = mm(later_all, wc_t[...]).astype(BF).reshape(lgr.shape)
 
     all_blocks(STK, stk_all, n - 1).wait_recv()
 
@@ -588,6 +590,7 @@
     scratch = [
         pltpu.VMEM(vf.shape, BF), pltpu.VMEM(results[1][0], BF), pltpu.VMEM(results[2][0], F32), pltpu.VMEM(results[3][0], F32),
         pltpu.VMEM((nb, up_rows, wb), F32), pltpu.VMEM((ch, (n + 2) * cells), BF),
+        pltpu.VMEM(wd.shape[::-1], BF), pltpu.VMEM(wc.shape, BF),
         pltpu.VMEM((6, rows + 2, width, ch), BF), pltpu.VMEM(four, BF), pltpu.VMEM(four, BF),
         pltpu.VMEM(we.shape, BF), pltpu.VMEM(wx.shape, BF), pltpu.VMEM(wd.shape, BF),
         pltpu.VMEM(wc.shape, BF), pltpu.VMEM(wu.shape, BF), pltpu.VMEM(perm.shape, BF),

time: 23.4 us -> 23.4 us (level)
  no operation moved by 1% of the time
where the time goes in v7:
time: 23.4 us; the launch traced here: 23.3 us
  Pallas kernels  22.6 us (97%)
  between operations  0.64 us (3%)
    pallas_call x1, Pallas kernels, shards(): pl.pallas_call(functools.partial(kernel, n, scale), out_shape=tuple((pltp...  21.8 us
    pallas_call x1, Pallas kernels, shards(): pl.pallas_call(tail, out_shape=tuple((jax.ShapeDtypeStruct(*result) for r...  0.8 us

profile of v7, /device:TPU:0, one launch (start us, length us, event | category | flops | bytes accessed | tf_op | source)
XLA Modules:
  0.0 23.3 jit_solution(9613938513900109422)
XLA Ops:
  0.6 21.8 %shard_map.128 = (bf16[2,12,8,256]{3,2,1,0:T(8,128)(2,1)S(1)}, bf16[1,6,4,256]{3,2,1,0:T(4,128)(2,1)S(1)}, f32[128,256]{1,0:T(8,128)S(1)}, f32[48,256]{1,0:T(8,128)S(1)}, bf16[16,16,128]{2,1,0:T(8,128)(2,1)S(1)}) custom-call(bf16[2,12,8,256]{3,2,1,0:T(8,128)(2,1)} %vf.1, bf16[2,12,8,256]{3,2,1,0:T(8,128)(2,1)} %ct.1, bf16[6912,256]{1,0:T(8,128)(2,1)} %we.1, ...), custom_call_target="tpu_custom_call" | custom-call | tf_op jit(solution)/shard_map/pallas_call | solution.py:614
  22.5 0.8 %shard_map.129 = (bf16[2,12,8,256]{3,2,1,0:T(8,128)(2,1)}, bf16[1,6,4,256]{3,2,1,0:T(4,128)(2,1)}, f32[128,256]{1,0:T(8,128)}, f32[48,256]{1,0:T(8,128)}, f32[16,2048]{1,0:T(8,128)}) custom-call(bf16[2,12,8,256]{3,2,1,0:T(8,128)(2,1)S(1)} %get-tuple-element.10.vg, bf16[1,6,4,256]{3,2,1,0:T(4,128)(2,1)S(1)} %get-tuple-element.11.code, ...), custom_call_target="tpu_custom_call" | custom-call | tf_op jit(solution)/shard_map/pallas_call | solution.py:622
